TPU v7x, 256 devices: a whole 4x4x8 slice. The times are simulated.
256 devices in a mesh: row: 8 (over z), col: 32 (over x, y, core).
Axes of the slice: x: 4, y: 4, z: 8, core: 2. Of those that a mesh axis runs over, the one named last changes fastest.
Arguments:
- rhs: float32 [64, 131072], P(None, ('row', 'col')), may hold values from -6 to 6
- pivots: int32 [4096], replicated, may hold values from 0 to 131071, as said below
- factor: float32 [4096, 1, 32, 128], P('row', None, 'col'), as said below
- diag_inv: float32 [8, 512, 512], P('row'), as said below
Outputs:
- solution: float32 [64, 1, 32, 128], P(None, None, 'col')
Inputs may be any that keep to these rules, and one draw needn't show every extreme that they name: `pivots`: distinct column numbers, the first 4096 entries of a permutation of 0 .. 131071. `factor`: entry (row i, column q) is zero where q >= 512 * (i // 512). `diag_inv`: each block is unit lower triangular.
All inputs are finite; a program needn't handle non-finite values.
Results may differ from a plain program's by a relative error of at most 0.0001.
Values sent between devices are 32-bit elements; how exact they have to be, the bound alone decides.
A program may use at most 64 MiB of HBM per device.

v0:
```python
import jax
import jax.numpy as jnp
from jax import lax
from jax.sharding import PartitionSpec as P


def in_blocks(shard, dim, peers):
    before, after = (shard.shape[:dim], shard.shape[dim + 1 :])
    return jnp.moveaxis(shard.reshape(*before, peers, -1, *after), dim, 0)


def summed_on_arrival(shard, axis, dim):
    peers = lax.axis_size(axis)
    pieces = lax.all_to_all(in_blocks(shard, dim, peers), axis, 0, 0, tiled=True)
    return jnp.sum(pieces, axis=0)


def from_everyone(shard, axis):
    peers = lax.axis_size(axis)
    return lax.all_to_all(
        jnp.broadcast_to(shard[None], (peers, *shard.shape)), axis, 0, 0, tiled=True
    )


def over_copies(shard, axis):
    return from_everyone(shard, axis).sum(axis=0)


def filled_up(lines, peers):
    spare = -lines.shape[0] % peers
    if not spare:
        return lines
    return jnp.concatenate([lines, jnp.zeros((spare, *lines.shape[1:]), lines.dtype)])


def in_order(pieces, dim):
    lengths = list(pieces.shape[1:])
    lengths[dim] *= pieces.shape[0]
    return jnp.moveaxis(pieces, 0, dim).reshape(lengths)


def gathered_copies(shard, axis, dim):
    pieces = from_everyone(shard, axis)
    return in_order(pieces, dim)


def sum_by_parts(shard, axes):
    lines = shard.reshape(-1, shard.shape[-1])
    padded = filled_up(lines, lax.axis_size(axes))
    whole = gathered_copies(summed_on_arrival(padded, axes, 0), axes, 0)
    return lax.slice_in_dim(whole, 0, len(lines)).reshape(shard.shape)


def from_root(shard, axis, root):
    return lax.dynamic_index_in_dim(lax.all_gather(shard, axis), root, 0, keepdims=False)


def apply_inverse(values, block_inv):
    return lax.dot_general(
        values,
        block_inv,
        (((1,), (1,)), ((), ())),
        precision=lax.Precision.HIGHEST,
        preferred_element_type=jnp.float32,
    )


def per_device(rhs, pivots, factor, diag_inv):
    my_row = lax.axis_index("row")
    my_col = lax.axis_index("col")
    col_count = lax.axis_size("col")
    rhs_count = rhs.shape[0]
    slab_rows = factor.shape[0]
    rounds = factor.shape[1]
    piece_len = factor.shape[3]
    block_len = diag_inv.shape[1]
    pieces = block_len // piece_len
    blocks_here = slab_rows // block_len
    total_blocks = blocks_here * lax.axis_size("row")
    first_column = (my_row * col_count + my_col) * rhs.shape[1]
    source_len = rhs.shape[1]
    located = pivots - first_column
    inside = (located >= 0) & (located < source_len)
    taken = jnp.take(rhs, jnp.clip(located, 0, source_len - 1), axis=1)
    taken = jnp.where(inside[None, :], taken, 0.0)
    permuted = summed_on_arrival(
        jnp.transpose(
            taken.reshape(rhs_count, blocks_here * lax.axis_size("row"), block_len), (1, 0, 2)
        ),
        "row",
        0,
    )
    permuted = over_copies(permuted, "col")
    factor_rows = factor.reshape(slab_rows, rounds * piece_len)

    def advance(number, solved):
        owner_row = number // blocks_here
        local_block = number % blocks_here
        partial_value = lax.dot_general(
            solved.reshape(rhs_count, rounds * piece_len),
            factor_rows,
            (((1,), (1,)), ((), ())),
            precision=lax.Precision.HIGHEST,
            preferred_element_type=jnp.float32,
        )
        own_rhs = lax.dynamic_index_in_dim(permuted, local_block, 0, keepdims=False)
        block_inv = lax.dynamic_index_in_dim(diag_inv, local_block, 0, keepdims=False)
        summed = sum_by_parts(partial_value, "col")
        fresh = apply_inverse(own_rhs - summed, block_inv)
        fresh = from_root(fresh, "row", owner_row)
        first_piece = number * pieces
        offset_piece = (my_col - first_piece) % col_count
        owns = offset_piece < pieces
        which = jnp.clip(offset_piece, 0, pieces - 1)
        local_round = jnp.clip((first_piece + offset_piece) // col_count, 0, rounds - 1)
        piece = lax.dynamic_slice_in_dim(fresh, which * piece_len, piece_len, 1)
        updated = lax.dynamic_update_index_in_dim(solved, piece[:, None, :], local_round, 1)
        return jnp.where(owns, updated, solved)

    start_state = jnp.zeros((rhs_count, rounds, 1, piece_len), jnp.float32)
    return lax.fori_loop(0, total_blocks, advance, start_state)


def solution(mesh):
    return jax.shard_map(
        per_device,
        mesh=mesh,
        in_specs=(P(None, ("row", "col")), P(), P("row", None, "col", None), P("row", None, None)),
        out_specs=P(None, None, "col", None),
        check_vma=False,
    )
```

profile of v0, /device:TPU:23, one launch (start us, length us, event | category | flops | bytes accessed | tf_op | source)
XLA Modules:
  0.0 625.0 jit_solution(16361289981323583431)
XLA Ops:
  8.1 1.0 copy.17
  9.1 10.8 %gather_fusion = f32[4096,64]{1,0:T(8,128)S(1)} fusion(f32[64,512]{0,1:T(8,128)S(1)} %copy.17, s32[4096]{0:T(1024)S(1)} %fusion.7), kind=kCustom, calls=%fused_computation | custom fusion | bytes 2113536 | tf_op jit(solution)/shard_map/jit(_take)/gather | solution.py:84
  20.7 35.3 %all_to_all.40 = f32[8,1,64,512]{3,2,1,0:T(8,128)S(1)} all-to-all(f32[8,1,64,512]{3,2,1,0:T(8,128)S(1)} %select_bitcast_fusion), channel_id=1, replica_groups=mesh['row'=8,'col'=32] {'row'}, dimensions={0} | all-to-all | bytes 2097152 | tf_op jit(solution)/shard_map/all_to_all | solution.py:14
  56.1 2.5 broadcast_in_dim.81
  58.6 9.4 %all-to-all-start.3 = ((f32[32,1,64,512]{3,2,1,0:T(8,128)}), f32[32,1,64,512]{3,2,1,0:T(8,128)}, u32[]{:S(2)}, u32[]{:S(2)}) async-start(f32[32,1,64,512]{3,2,1,0:T(8,128)} %broadcast_in_dim.81), calls=%async_computation.3 | async-start | bytes 8388608 | tf_op jit(solution)/shard_map/all_to_all | solution.py:20
  68.0 51.4 %all-to-all-done.3 = f32[32,1,64,512]{3,2,1,0:T(8,128)} async-done(((f32[32,1,64,512]{3,2,1,0:T(8,128)}), f32[32,1,64,512]{3,2,1,0:T(8,128)}, u32[]{:S(2)}, u32[]{:S(2)}) %all-to-all-start.3) | async-done | bytes 4194336 | tf_op jit(solution)/shard_map/all_to_all | solution.py:20
  119.4 2.5 reduce_sum.38
  122.0 495.6 %while.17 = (s32[]{:T(128)}, f32[64,1,1,128]{3,0,2,1:T(8,128)S(1)}, s32[]{:T(128)}, f32[512,128]{1,0:T(8,128)S(1)}, f32[1,64,512]{2,1,0:T(8,128)S(1)}, /*index=5...) while((s32[]{:T(128)}, f32[64,1,1,128]{3,0,2,1:T(8,128)S(1)}, ...), condition=%wide.region_4.5_spmd.clone, body=%wide.region_2.4_spmd.clone.sunk | while | flops 251747328 | bytes 6889937 | solution.py:121
  122.5 11.5 %all_to_all.41 = f32[32,2,512]{2,1,0:T(2,128)S(1)} all-to-all(f32[32,2,512]{2,1,0:T(2,128)S(1)} %copy.28), channel_id=1, replica_groups=mesh['row'=8,'col'=32] {'col'}, dimensions={0} | all-to-all | bytes 262144 | tf_op jit(solution)/shard_map/while/body/eval_jaxpr/all_to_all | solution.py:14
  134.1 11.2 %all_to_all.42 = f32[32,2,512]{2,1,0:T(2,128)S(1)} all-to-all(f32[32,2,512]{2,1,0:T(2,128)S(1)} %broadcast_in_dim.89), channel_id=1, replica_groups=mesh['row'=8,'col'=32] {'col'}, dimensions={0} | all-to-all | bytes 262144 | tf_op jit(solution)/shard_map/while/body/eval_jaxpr/all_to_all | solution.py:20
  145.4 1.8 fusion.19
  147.3 29.4 %all-gather.6.cloned.1.call-done = f32[512,512]{1,0:T(8,128)} async-done(((f32[64,512]{1,0:T(8,128)}), f32[512,512]{1,0:T(8,128)}) %all-gather.6.cloned.1.call-update) | async-done | bytes 1048592 | tf_op jit(solution)/shard_map/while/body/eval_jaxpr/all_gather | solution.py:55
  176.7 0.8 bitcast_select_fusion.2
  178.1 16.5 %all_to_all.41 = f32[32,2,512]{2,1,0:T(2,128)S(1)} all-to-all(f32[32,2,512]{2,1,0:T(2,128)S(1)} %copy.28), channel_id=1, replica_groups=mesh['row'=8,'col'=32] {'col'}, dimensions={0} | all-to-all | bytes 262144 | tf_op jit(solution)/shard_map/while/body/eval_jaxpr/all_to_all | solution.py:14
  194.7 11.2 %all_to_all.42 = f32[32,2,512]{2,1,0:T(2,128)S(1)} all-to-all(f32[32,2,512]{2,1,0:T(2,128)S(1)} %broadcast_in_dim.89), channel_id=1, replica_groups=mesh['row'=8,'col'=32] {'col'}, dimensions={0} | all-to-all | bytes 262144 | tf_op jit(solution)/shard_map/while/body/eval_jaxpr/all_to_all | solution.py:20
  206.0 1.8 fusion.19
  207.8 31.7 %all-gather.6.cloned.1.call-done = f32[512,512]{1,0:T(8,128)} async-done(((f32[64,512]{1,0:T(8,128)}), f32[512,512]{1,0:T(8,128)}) %all-gather.6.cloned.1.call-update) | async-done | bytes 1048592 | tf_op jit(solution)/shard_map/while/body/eval_jaxpr/all_gather | solution.py:55
  239.5 0.8 bitcast_select_fusion.2
  240.9 16.5 %all_to_all.41 = f32[32,2,512]{2,1,0:T(2,128)S(1)} all-to-all(f32[32,2,512]{2,1,0:T(2,128)S(1)} %copy.28), channel_id=1, replica_groups=mesh['row'=8,'col'=32] {'col'}, dimensions={0} | all-to-all | bytes 262144 | tf_op jit(solution)/shard_map/while/body/eval_jaxpr/all_to_all | solution.py:14
  257.5 11.2 %all_to_all.42 = f32[32,2,512]{2,1,0:T(2,128)S(1)} all-to-all(f32[32,2,512]{2,1,0:T(2,128)S(1)} %broadcast_in_dim.89), channel_id=1, replica_groups=mesh['row'=8,'col'=32] {'col'}, dimensions={0} | all-to-all | bytes 262144 | tf_op jit(solution)/shard_map/while/body/eval_jaxpr/all_to_all | solution.py:20
  268.8 1.8 fusion.19
  270.7 31.7 %all-gather.6.cloned.1.call-done = f32[512,512]{1,0:T(8,128)} async-done(((f32[64,512]{1,0:T(8,128)}), f32[512,512]{1,0:T(8,128)}) %all-gather.6.cloned.1.call-update) | async-done | bytes 1048592 | tf_op jit(solution)/shard_map/while/body/eval_jaxpr/all_gather | solution.py:55
  302.4 0.8 bitcast_select_fusion.2
  303.7 16.5 %all_to_all.41 = f32[32,2,512]{2,1,0:T(2,128)S(1)} all-to-all(f32[32,2,512]{2,1,0:T(2,128)S(1)} %copy.28), channel_id=1, replica_groups=mesh['row'=8,'col'=32] {'col'}, dimensions={0} | all-to-all | bytes 262144 | tf_op jit(solution)/shard_map/while/body/eval_jaxpr/all_to_all | solution.py:14
  320.3 11.2 %all_to_all.42 = f32[32,2,512]{2,1,0:T(2,128)S(1)} all-to-all(f32[32,2,512]{2,1,0:T(2,128)S(1)} %broadcast_in_dim.89), channel_id=1, replica_groups=mesh['row'=8,'col'=32] {'col'}, dimensions={0} | all-to-all | bytes 262144 | tf_op jit(solution)/shard_map/while/body/eval_jaxpr/all_to_all | solution.py:20
  331.7 1.8 fusion.19
  333.5 31.7 %all-gather.6.cloned.1.call-done = f32[512,512]{1,0:T(8,128)} async-done(((f32[64,512]{1,0:T(8,128)}), f32[512,512]{1,0:T(8,128)}) %all-gather.6.cloned.1.call-update) | async-done | bytes 1048592 | tf_op jit(solution)/shard_map/while/body/eval_jaxpr/all_gather | solution.py:55
  365.2 0.8 bitcast_select_fusion.2
  366.6 16.5 %all_to_all.41 = f32[32,2,512]{2,1,0:T(2,128)S(1)} all-to-all(f32[32,2,512]{2,1,0:T(2,128)S(1)} %copy.28), channel_id=1, replica_groups=mesh['row'=8,'col'=32] {'col'}, dimensions={0} | all-to-all | bytes 262144 | tf_op jit(solution)/shard_map/while/body/eval_jaxpr/all_to_all | solution.py:14
  383.2 11.2 %all_to_all.42 = f32[32,2,512]{2,1,0:T(2,128)S(1)} all-to-all(f32[32,2,512]{2,1,0:T(2,128)S(1)} %broadcast_in_dim.89), channel_id=1, replica_groups=mesh['row'=8,'col'=32] {'col'}, dimensions={0} | all-to-all | bytes 262144 | tf_op jit(solution)/shard_map/while/body/eval_jaxpr/all_to_all | solution.py:20
  394.5 1.8 fusion.19
  396.3 31.7 %all-gather.6.cloned.1.call-done = f32[512,512]{1,0:T(8,128)} async-done(((f32[64,512]{1,0:T(8,128)}), f32[512,512]{1,0:T(8,128)}) %all-gather.6.cloned.1.call-update) | async-done | bytes 1048592 | tf_op jit(solution)/shard_map/while/body/eval_jaxpr/all_gather | solution.py:55
  428.0 0.8 bitcast_select_fusion.2
  429.4 16.5 %all_to_all.41 = f32[32,2,512]{2,1,0:T(2,128)S(1)} all-to-all(f32[32,2,512]{2,1,0:T(2,128)S(1)} %copy.28), channel_id=1, replica_groups=mesh['row'=8,'col'=32] {'col'}, dimensions={0} | all-to-all | bytes 262144 | tf_op jit(solution)/shard_map/while/body/eval_jaxpr/all_to_all | solution.py:14
  446.0 11.2 %all_to_all.42 = f32[32,2,512]{2,1,0:T(2,128)S(1)} all-to-all(f32[32,2,512]{2,1,0:T(2,128)S(1)} %broadcast_in_dim.89), channel_id=1, replica_groups=mesh['row'=8,'col'=32] {'col'}, dimensions={0} | all-to-all | bytes 262144 | tf_op jit(solution)/shard_map/while/body/eval_jaxpr/all_to_all | solution.py:20
  457.3 1.8 fusion.19
  459.2 31.7 %all-gather.6.cloned.1.call-done = f32[512,512]{1,0:T(8,128)} async-done(((f32[64,512]{1,0:T(8,128)}), f32[512,512]{1,0:T(8,128)}) %all-gather.6.cloned.1.call-update) | async-done | bytes 1048592 | tf_op jit(solution)/shard_map/while/body/eval_jaxpr/all_gather | solution.py:55
  490.9 0.8 bitcast_select_fusion.2
  492.2 16.6 %all_to_all.41 = f32[32,2,512]{2,1,0:T(2,128)S(1)} all-to-all(f32[32,2,512]{2,1,0:T(2,128)S(1)} %copy.28), channel_id=1, replica_groups=mesh['row'=8,'col'=32] {'col'}, dimensions={0} | all-to-all | bytes 262144 | tf_op jit(solution)/shard_map/while/body/eval_jaxpr/all_to_all | solution.py:14
  508.9 11.2 %all_to_all.42 = f32[32,2,512]{2,1,0:T(2,128)S(1)} all-to-all(f32[32,2,512]{2,1,0:T(2,128)S(1)} %broadcast_in_dim.89), channel_id=1, replica_groups=mesh['row'=8,'col'=32] {'col'}, dimensions={0} | all-to-all | bytes 262144 | tf_op jit(solution)/shard_map/while/body/eval_jaxpr/all_to_all | solution.py:20
  520.3 1.8 fusion.19
  522.1 31.7 %all-gather.6.cloned.1.call-done = f32[512,512]{1,0:T(8,128)} async-done(((f32[64,512]{1,0:T(8,128)}), f32[512,512]{1,0:T(8,128)}) %all-gather.6.cloned.1.call-update) | async-done | bytes 1048592 | tf_op jit(solution)/shard_map/while/body/eval_jaxpr/all_gather | solution.py:55
  553.8 0.8 bitcast_select_fusion.2
  555.2 16.5 %all_to_all.41 = f32[32,2,512]{2,1,0:T(2,128)S(1)} all-to-all(f32[32,2,512]{2,1,0:T(2,128)S(1)} %copy.28), channel_id=1, replica_groups=mesh['row'=8,'col'=32] {'col'}, dimensions={0} | all-to-all | bytes 262144 | tf_op jit(solution)/shard_map/while/body/eval_jaxpr/all_to_all | solution.py:14
  571.8 11.2 %all_to_all.42 = f32[32,2,512]{2,1,0:T(2,128)S(1)} all-to-all(f32[32,2,512]{2,1,0:T(2,128)S(1)} %broadcast_in_dim.89), channel_id=1, replica_groups=mesh['row'=8,'col'=32] {'col'}, dimensions={0} | all-to-all | bytes 262144 | tf_op jit(solution)/shard_map/while/body/eval_jaxpr/all_to_all | solution.py:20
  583.1 1.8 fusion.19
  584.9 31.7 %all-gather.6.cloned.1.call-done = f32[512,512]{1,0:T(8,128)} async-done(((f32[64,512]{1,0:T(8,128)}), f32[512,512]{1,0:T(8,128)}) %all-gather.6.cloned.1.call-update) | async-done | bytes 1048592 | tf_op jit(solution)/shard_map/while/body/eval_jaxpr/all_gather | solution.py:55
  616.6 0.9 bitcast_select_fusion.2
  (78 shorter events, 8.8 us)
Async XLA Ops:
  58.6 60.8 %all-to-all-start.3 = ((f32[32,1,64,512]{3,2,1,0:T(8,128)}), f32[32,1,64,512]{3,2,1,0:T(8,128)}, u32[]{:S(2)}, u32[]{:S(2)}) async-start(f32[32,1,64,512]{3,2,1,0:T(8,128)} %broadcast_in_dim.81), calls=%async_computation.3 | async-start | bytes 8388608 | tf_op jit(solution)/shard_map/all_to_all | solution.py:20
  68.0 53.9 %copy-start = (f32[1,512,512]{2,1,0:T(8,128)S(1)}, f32[1,512,512]{2,1,0:T(8,128)}, u32[]{:S(2)}) copy-start(f32[1,512,512]{2,1,0:T(8,128)} %param.9) | copy-start | bytes 3145732
  68.0 53.9 %copy-start.1 = (f32[512,1,1,128]{3,2,1,0:T(1,128)S(1)}, f32[512,1,1,128]{3,2,1,0:T(1,128)}, u32[]{:S(2)}) copy-start(f32[512,1,1,128]{3,2,1,0:T(1,128)} %param.8) | copy-start | bytes 786436
  122.0 54.7 %all-gather.6.cloned.1.call-start = ((), (), s32[]{:S(2)}) async-start(), calls=%async_computation.4 | async-start | bytes 1179648 | tf_op jit(solution)/shard_map/while/body/eval_jaxpr/all_gather | solution.py:55
  177.5 62.0 %all-gather.6.cloned.1.call-start = ((), (), s32[]{:S(2)}) async-start(), calls=%async_computation.4 | async-start | bytes 1179648 | tf_op jit(solution)/shard_map/while/body/eval_jaxpr/all_gather | solution.py:55
  240.4 62.0 %all-gather.6.cloned.1.call-start = ((), (), s32[]{:S(2)}) async-start(), calls=%async_computation.4 | async-start | bytes 1179648 | tf_op jit(solution)/shard_map/while/body/eval_jaxpr/all_gather | solution.py:55
  303.2 62.0 %all-gather.6.cloned.1.call-start = ((), (), s32[]{:S(2)}) async-start(), calls=%async_computation.4 | async-start | bytes 1179648 | tf_op jit(solution)/shard_map/while/body/eval_jaxpr/all_gather | solution.py:55
  366.0 62.0 %all-gather.6.cloned.1.call-start = ((), (), s32[]{:S(2)}) async-start(), calls=%async_computation.4 | async-start | bytes 1179648 | tf_op jit(solution)/shard_map/while/body/eval_jaxpr/all_gather | solution.py:55
  428.9 62.0 %all-gather.6.cloned.1.call-start = ((), (), s32[]{:S(2)}) async-start(), calls=%async_computation.4 | async-start | bytes 1179648 | tf_op jit(solution)/shard_map/while/body/eval_jaxpr/all_gather | solution.py:55
  491.7 62.1 %all-gather.6.cloned.1.call-start = ((), (), s32[]{:S(2)}) async-start(), calls=%async_computation.4 | async-start | bytes 1179648 | tf_op jit(solution)/shard_map/while/body/eval_jaxpr/all_gather | solution.py:55
  554.6 62.0 %all-gather.6.cloned.1.call-start = ((), (), s32[]{:S(2)}) async-start(), calls=%async_computation.4 | async-start | bytes 1179648 | tf_op jit(solution)/shard_map/while/body/eval_jaxpr/all_gather | solution.py:55
  617.5 0.6 copy-start.2
Sparse Core Ops, SparseCore 0:
  147.3 29.2 all-gather.5
  207.9 31.5 all-gather.5
  270.7 31.5 all-gather.5
  333.6 31.5 all-gather.5
  396.4 31.5 all-gather.5
  459.3 31.5 all-gather.5
  522.2 31.5 all-gather.5
  585.0 31.5 all-gather.5
where the time goes:
time: 632 us; the launch traced here: 625 us
  waiting for transfers between devices  303 us (48%)
  blocking collectives  252 us (40%)
  local copies, waits for them, and re-layouts  17.4 us (3%)
  matrix products  17.2 us (3%)
  between operations  13.5 us (2%)
  other arithmetic  11.5 us (2%)
  starting transfers between devices  9.64 us (2%)
    all_gather x8, waiting for transfers between devices, from_root(): lax.all_gather(shard, axis)  251 us
    all_to_all x9, blocking collectives, summed_on_arrival(): lax.all_to_all(in_blocks(shard, dim, peers), axis, 0, 0, tiled=True)  162 us
    all_to_all x8, blocking collectives, from_everyone(): lax.all_to_all(jnp.broadcast_to(shard[None], (peers, *shard.shape)), axis...  90 us
    all_to_all x1, waiting for transfers between devices, from_everyone(): lax.all_to_all(jnp.broadcast_to(shard[None], (peers, *shard.shape)), axis...  51.4 us
    dot_general x8, matrix products, apply_inverse(): lax.dot_general(values, block_inv, (((1,), (1,)), ((), ())), precision=la...  14.1 us
  transfers between devices with their start and end apart: 9, of which 9 were waited for; matrix products, arithmetic and copies ran while one was open for 0% of the time, Pallas kernels for 0%

commit v1 on v0

v1 whole, which is shorter than its diff:
```python
import functools

import jax
import jax.numpy as jnp
from jax import lax
from jax.experimental import pallas as pl
from jax.experimental.pallas import tpu as pltpu
from jax.sharding import PartitionSpec as P

MESH = pl.DeviceIdType.MESH
NX, NY = 4, 4
CHIPS = NX * NY
COLS = 2 * CHIPS
ROWS = 8
BLK = 512
CB = 128
NRHS = 64
G = NRHS // CHIPS
CHAIN, GATHER = 1, 0
BF16, F32 = jnp.bfloat16, jnp.float32


def split(v):
    hi = v.astype(BF16)
    lo = (v - hi.astype(F32)).astype(BF16)
    return hi, lo


def packed(v):
    return jnp.concatenate([v[:, : BLK // 2], v[:, BLK // 2 :]], axis=0)


def unpacked(v):
    return jnp.concatenate([v[:G], v[G:]], axis=1)


def times_t(v, hi_ref, lo_ref):
    hi, lo = split(v)
    lhs = jnp.concatenate([hi.astype(F32), lo.astype(F32)], axis=0).astype(BF16)
    dims = (((1,), (1,)), ((), ()))
    o = lax.dot_general(lhs, hi_ref[...], dims, preferred_element_type=F32)
    o = o + lax.dot_general(lhs, lo_ref[...], dims, preferred_element_type=F32)
    return o[:G] + o[G:]


def kernel(
    rhs_ref, piv_ref, l_ref, d_ref, out_ref,
    s1_send, s1_recv, s2_send, s2_recv, e2, x2, ybuf, acc, pbuf, orecv, lall, bhi, blo, dhi, dlo,
    s1_ssem, s1_rsem, s2_ssem, s2_rsem, y_ssem, y_rsem, o_ssem, o_rsem, g_ssem, g_rsem, b_ssem,
):
    row = lax.axis_index("row")
    col = lax.axis_index("col")
    chip, core = col // 2, col % 2
    x, y = chip // NY, chip % NY
    is_chain = core == CHAIN
    is_gather = core == GATHER

    def chain_col(c):
        return 2 * c + CHAIN

    def remote(src, dst, ssem, rsem, dev):
        return pltpu.make_async_remote_copy(
            src_ref=src, dst_ref=dst, send_sem=ssem, recv_sem=rsem, device_id=dev, device_id_type=MESH
        )

    barrier = pltpu.get_barrier_semaphore()

    def greet_plane(i, _):
        pl.semaphore_signal(barrier, inc=1, device_id=(row, lax.rem(col + i, COLS)), device_id_type=MESH)
        return 0

    def greet_z(i, _):
        pl.semaphore_signal(barrier, inc=1, device_id=(lax.rem(row + i, ROWS), col), device_id_type=MESH)
        return 0

    lax.fori_loop(1, COLS, greet_plane, 0)

    @pl.when(is_chain)
    def _():
        lax.fori_loop(1, ROWS, greet_z, 0)

    for c in range(CHIPS):
        for q in range(4):
            s1_send[c, G * q : G * q + G, :] = rhs_ref[G * c : G * c + G, CB * q : CB * q + CB]

    @pl.when(is_chain)
    def _():
        pl.semaphore_wait(barrier, COLS - 1 + ROWS - 1)

    @pl.when(is_gather)
    def _():
        pl.semaphore_wait(barrier, COLS - 1)

    def send_s1(i, _):
        c = lax.rem(chip + i, CHIPS)
        remote(s1_send.at[c], s1_recv.at[col], s1_ssem, s1_rsem, (row, chain_col(c))).start()
        return 0

    @pl.when(is_gather)
    def _():
        lax.fori_loop(0, CHIPS, send_s1, 0)

    @pl.when(is_chain)
    def _():
        s1_recv[col] = s1_send[chip]
        lax.fori_loop(1, CHIPS, send_s1, 0)

    me_chain = (row, chain_col(chip))

    def flow_cols(f, du, dv):
        dx, dy = (du, dv) if f == 0 else (dv, du)
        return lax.rem(x + dx, NX) * NY + lax.rem(y + dy, NY)

    def gather_plan(f):
        up, un, vp, vn = (1, 0), (3, 0), (0, 1), (0, 3)
        own = [(up, True), (un, True), (vp, True), (vn, False)]
        return [
            ((0, 0), own),
            ((1, 0), [(up, True), (vp, True), (vn, False)]),
            ((3, 0), [(vn, True), (vp, False)]),
            ((0, 1), [(vp, False)]),
            ((2, 0), [(vn, True), (vp, False)]),
            ((1, 1), [(vp, False)]),
            ((3, 3), [(vn, False)]),
            ((2, 3), [(vn, False)]),
        ]

    def gather_events(do):
        plans = [gather_plan(0), gather_plan(1)]
        n = 0
        for e in range(len(plans[0])):
            for f in (0, 1):
                (su, sv), sends = plans[f][e]
                src_chip = flow_cols(f, (4 - su) % 4, (4 - sv) % 4)
                live = src_chip < 2 * row
                do(f, e, src_chip, live, sends, n)
                n += 1 + len(sends)

    def copies_of(f, e, src_chip, sends, n):
        src = l_ref if (f == GATHER and e == 0) else lall.at[src_chip, f]
        out = []
        for k, ((du, dv), to_gather) in enumerate(sends):
            dest = flow_cols(f, du, dv) * 2 + (GATHER if to_gather else CHAIN)
            out.append(remote(src, lall.at[src_chip, f], g_ssem.at[n + k], g_rsem.at[src_chip, f], (row, dest)))
        out.append(remote(src, lall.at[src_chip, f], g_ssem.at[n + len(sends)], g_rsem.at[src_chip, f], me_chain))
        return out

    def l_piece_wait(a, f):
        remote(lall.at[a, f], lall.at[a, f], b_ssem, g_rsem.at[a, f], me_chain).wait_recv()

    @pl.when(is_gather)
    def _():
        def do(f, e, src_chip, live, sends, n):
            @pl.when(live)
            def _():
                if not (f == GATHER and e == 0):
                    l_piece_wait(src_chip, f)
                for c in copies_of(f, e, src_chip, sends, n):
                    c.start()

        gather_events(do)

        def done(f, e, src_chip, live, sends, n):
            @pl.when(live)
            def _():
                for c in copies_of(f, e, src_chip, sends, n):
                    c.wait_send()

        gather_events(done)
        remote(s1_send, s1_send, s1_ssem, s1_rsem, me_chain).wait_send()
        remote(orecv, orecv, b_ssem, o_rsem, me_chain).wait_recv()

    @pl.when(is_chain)
    def _():
        partner = (row, 2 * chip + GATHER)
        own_live = chip < 2 * row

        @pl.when(own_live)
        def _():
            remote(l_ref, lall.at[chip, CHAIN], b_ssem, g_rsem.at[chip, CHAIN], partner).start()

        d = d_ref[...]
        hi, lo = split(d)
        dhi[...] = hi
        dlo[...] = lo

        width = COLS * BLK
        piv = piv_ref[...] - row * width
        low = jnp.broadcast_to(piv & (CB - 1), (CB, ROWS * BLK))
        hot = (lax.broadcasted_iota(jnp.int32, (CB, ROWS * BLK), 0) == low).astype(F32).astype(BF16)
        e2[0:CB, :] = hot
        e2[CB:, :] = hot

        remote(s1_recv.at[pl.ds(0, COLS - 1)], s1_recv.at[pl.ds(0, COLS - 1)], b_ssem, s1_rsem, partner).wait_recv()
        v = s1_recv[...].reshape(COLS * 4 * G, CB)
        hi, lo = split(v)
        x2[:, 0:CB] = hi
        x2[:, CB:] = lo

        def select(j, _):
            off = pl.multiple_of(j * BLK, BLK)
            t = jnp.dot(x2[...], e2[:, pl.ds(off, BLK)], preferred_element_type=F32)
            high = jnp.right_shift(piv_ref[:, pl.ds(off, BLK)] - row * width, 7)
            rows_hi = jnp.right_shift(lax.broadcasted_iota(jnp.int32, (COLS * 4 * G, BLK), 0), 2)
            t = jnp.where(rows_hi == jnp.broadcast_to(high, rows_hi.shape), t, 0.0)
            t = jnp.sum(t.reshape(COLS * 4 * G // 8, 8, BLK), axis=0)
            tile = packed(t[:G] + t[G:])

            @pl.when(j == row)
            def _():
                s2_recv[row] = tile

            @pl.when(j != row)
            def _():
                s2_send[j] = tile
                remote(s2_send.at[j], s2_recv.at[row], s2_ssem, s2_rsem, (j, col)).start()

            return 0

        lax.fori_loop(0, ROWS, select, 0)
        remote(s2_recv.at[pl.ds(0, ROWS - 1)], s2_recv.at[pl.ds(0, ROWS - 1)], b_ssem, s2_rsem, partner).wait_recv()
        pbuf[...] = unpacked(jnp.sum(s2_recv[...], axis=0))
        acc[...] = jnp.zeros_like(acc)

        def finish():
            fresh = times_t(pbuf[...] - acc[...], dhi, dlo)
            ybuf[row] = packed(fresh)
            for i in range(1, ROWS):
                remote(ybuf.at[row], ybuf.at[row], y_ssem, y_rsem.at[row], (lax.rem(row + i, ROWS), col)).start()

        @pl.when(row == 0)
        def _():
            finish()

        def step(m, _):
            @pl.when(m < row)
            def _():
                for t in range(4):
                    l_piece_wait(2 * m + t // 2, t % 2)
                for t in range(4):
                    hi, lo = split(lall[2 * m + t // 2, t % 2])
                    bhi[:, CB * t : CB * t + CB] = hi
                    blo[:, CB * t : CB * t + CB] = lo

            @pl.when(m != row)
            def _():
                remote(ybuf.at[m], ybuf.at[m], b_ssem, y_rsem.at[m], partner).wait_recv()

            @pl.when(m < row)
            def _():
                acc[...] += times_t(unpacked(ybuf[m]), bhi, blo)

            @pl.when(m + 1 == row)
            def _():
                finish()

            for t in range(4):
                lanes = pl.ds(CB * (t % 2), CB)
                dest = 4 * m + t

                @pl.when(dest == col)
                def _():
                    orecv[chip] = ybuf[m, :, lanes]

                @pl.when(dest != col)
                def _():
                    remote(ybuf.at[m, :, lanes], orecv.at[chip], o_ssem.at[m], o_rsem, (row, dest)).start()

            return 0

        lax.fori_loop(0, ROWS, step, 0)

        @pl.when(own_live)
        def _():
            remote(l_ref, lall.at[chip, CHAIN], b_ssem, g_rsem.at[chip, CHAIN], partner).wait_send()

        remote(s1_send.at[pl.ds(0, CHIPS - 1)], s1_send.at[pl.ds(0, CHIPS - 1)], s1_ssem, s1_rsem, partner).wait_send()
        remote(s2_send.at[pl.ds(0, ROWS - 1)], s2_send.at[pl.ds(0, ROWS - 1)], s2_ssem, s2_rsem, partner).wait_send()
        remote(ybuf.at[pl.ds(0, ROWS - 1)], ybuf.at[pl.ds(0, ROWS - 1)], y_ssem, y_rsem.at[row], partner).wait_send()

        def drain(m, _):
            @pl.when(m == col // 4)
            def _():
                remote(orecv.at[pl.ds(0, 3)], orecv.at[pl.ds(0, 3)], o_ssem.at[m], o_rsem, partner).wait_send()

            @pl.when(m != col // 4)
            def _():
                remote(orecv.at[pl.ds(0, 4)], orecv.at[pl.ds(0, 4)], o_ssem.at[m], o_rsem, partner).wait_send()

            return 0

        lax.fori_loop(0, ROWS, drain, 0)
        remote(
            orecv.at[pl.ds(0, CHIPS - 1)], orecv.at[pl.ds(0, CHIPS - 1)], b_ssem, o_rsem, partner
        ).wait_recv()

    upper = lax.rem(chip, 2) == 0
    for c in range(CHIPS):
        tile = orecv[c]
        out_ref[G * c : G * c + G, :] = jnp.where(upper, tile[:G], tile[G:])


def per_device(rhs, pivots, factor, diag_inv):
    vmem = pl.BlockSpec(memory_space=pltpu.VMEM)
    dma = pltpu.SemaphoreType.DMA
    out = pl.pallas_call(
        kernel,
        out_shape=jax.ShapeDtypeStruct((NRHS, CB), F32),
        in_specs=[vmem] * 4,
        out_specs=vmem,
        scratch_shapes=[
            pltpu.VMEM((CHIPS, 4 * G, CB), F32),
            pltpu.VMEM((COLS, 4 * G, CB), F32),
            pltpu.VMEM((ROWS, 8, BLK // 2), F32),
            pltpu.VMEM((ROWS, 8, BLK // 2), F32),
            pltpu.VMEM((2 * CB, ROWS * BLK), BF16),
            pltpu.VMEM((COLS * 4 * G, 2 * CB), BF16),
            pltpu.VMEM((ROWS, 8, BLK // 2), F32),
            pltpu.VMEM((G, BLK), F32),
            pltpu.VMEM((G, BLK), F32),
            pltpu.VMEM((CHIPS, 8, CB), F32),
            pltpu.VMEM((CHIPS, 2, BLK, CB), F32),
            pltpu.VMEM((BLK, BLK), BF16),
            pltpu.VMEM((BLK, BLK), BF16),
            pltpu.VMEM((BLK, BLK), BF16),
            pltpu.VMEM((BLK, BLK), BF16),
            dma, dma, dma, dma, dma,
            dma((ROWS,)),
            dma((ROWS,)),
            dma,
            dma((48,)),
            dma((CHIPS, 2)),
            dma,
        ],
        compiler_params=pltpu.CompilerParams(
            collective_id=0, has_side_effects=True, vmem_limit_bytes=56 * 1024 * 1024
        ),
    )(
        rhs,
        pivots.reshape(1, ROWS * BLK),
        factor.reshape(BLK, CB),
        diag_inv.reshape(BLK, BLK),
    )
    return out.reshape(NRHS, 1, 1, CB)


def solution(mesh):
    return jax.shard_map(
        per_device,
        mesh=mesh,
        in_specs=(P(None, ("row", "col")), P(), P("row", None, "col", None), P("row", None, None)),
        out_specs=P(None, None, "col", None),
        check_vma=False,
    )
```

time: 632 us -> 56.9 us (0.09); the launches traced: 625 us -> 56.8 us
  waiting for transfers between devices: 303 us -> 0 us
  blocking collectives: 252 us -> 0 us
  Pallas kernels: 0 us -> 55.4 us
  matrix products: 17.2 us -> 0 us
  local copies, waits for them, and re-layouts: 17.4 us -> 1.38 us
  between operations: 13.5 us -> 0.01 us
  other arithmetic: 11.5 us -> 0 us
  starting transfers between devices: 9.64 us -> 0 us
    all_to_all x17 -> x0, blocking collectives: 252 us -> none  [the longest x9 162 us: summed_on_arrival(): lax.all_to_all(in_blocks(shard, dim, peers), axis, 0, 0, tiled=True)]
    all_gather x8 -> x0, waiting for transfers between devices: 251 us -> none  [from_root(): lax.all_gather(shard, axis)]
    pallas_call x0 -> x1, Pallas kernels: none -> 55.4 us  [per_device(): pl.pallas_call(kernel, out_shape=jax.ShapeDtypeStruct((NRHS, CB), F32), i...]
    all_to_all x1 -> x0, waiting for transfers between devices: 51.4 us -> none  [from_everyone(): lax.all_to_all(jnp.broadcast_to(shard[None], (peers, *shard.shape)), axis...]
    dot_general x16 -> x0, matrix products: 17.2 us -> none  [the longest x8 14.1 us: apply_inverse(): lax.dot_general(values, block_inv, (((1,), (1,)), ((), ())), precision=la...]
    gather x2 -> x0, local copies, waits for them, and re-layouts: 11.4 us -> none  [per_device(): taken = jnp.take(rhs, jnp.clip(located, 0, source_len - 1), axis=1)]
    all_to_all x1 -> x0, starting transfers between devices: 9.41 us -> none  [from_everyone(): lax.all_to_all(jnp.broadcast_to(shard[None], (peers, *shard.shape)), axis...]
    select_n x8 -> x0, other arithmetic: 6.75 us -> none  [advance(): return jnp.where(owns, updated, solved)]
  transfers between devices with their start and end apart: 9 -> 0, of which waited for: 9 -> 0; matrix products, arithmetic and copies ran while one was open for 0% -> 0% of each run, Pallas kernels for 0% -> 0%
where the time goes in v1:
time: 56.9 us; the launch traced here: 56.8 us
  Pallas kernels  55.4 us (97%)
  local copies, waits for them, and re-layouts  1.38 us (2%)
    pallas_call x1, Pallas kernels, per_device(): pl.pallas_call(kernel, out_shape=jax.ShapeDtypeStruct((NRHS, CB), F32), i...  55.4 us
    unnamed x1, local copies, waits for them, and re-layouts  1.38 us

profile of v1, /device:TPU:23, one launch (start us, length us, event | category | flops | bytes accessed | tf_op | source)
XLA Modules:
  0.0 56.8 jit_solution(16360936762366080438)
XLA Ops:
  0.0 55.4 %shard_map.46 = f32[64,128]{1,0:T(8,128)} custom-call(f32[64,512]{1,0:T(8,128)} %rhs_ref.1, s32[1,4096]{1,0:T(1,128)} %bitcast.9, f32[512,128]{1,0:T(8,128)} %bitcast.7, f32[512,512]{1,0:T(8,128)} %bitcast.6), custom_call_target="tpu_custom_call" | custom-call | tf_op jit(solution)/shard_map/pallas_call | solution.py:306
  55.4 1.4 %copy.7 = f32[64,1,1,128]{3,2,1,0:T(1,128)} copy(f32[64,1,1,128]{3,2,1,0:T(1,128)} %bitcast.8) | data formatting | bytes 65536

commit v2 on v1

--- a/solution.py
+++ b/solution.py
@@ -18,6 +18,8 @@
 G = NRHS // CHIPS
 CHAIN, GATHER = 1, 0
 BF16, F32 = jnp.bfloat16, jnp.float32
+CHUNKS = 4
+ROWS_C = BLK // CHUNKS
 
 
 def split(v):
@@ -45,7 +47,7 @@
 
 def kernel(
     rhs_ref, piv_ref, l_ref, d_ref, out_ref,
-    s1_send, s1_recv, s2_send, s2_recv, e2, x2, ybuf, acc, pbuf, orecv, lall, bhi, blo, dhi, dlo,
+    s1_send, s1_recv, s2_send, s2_recv, e2, xhi, xlo, ybuf, acc, pbuf, orecv, lall, bhi, blo, dhi, dlo,
     s1_ssem, s1_rsem, s2_ssem, s2_rsem, y_ssem, y_rsem, o_ssem, o_rsem, g_ssem, g_rsem, b_ssem,
 ):
     row = lax.axis_index("row")
@@ -81,7 +83,8 @@
 
     for c in range(CHIPS):
         for q in range(4):
-            s1_send[c, G * q : G * q + G, :] = rhs_ref[G * c : G * c + G, CB * q : CB * q + CB]
+            at = 2 * G * (q % 2) + G * (q // 2)
+            s1_send[c, at : at + G, :] = rhs_ref[G * c : G * c + G, CB * q : CB * q + CB]
 
     @pl.when(is_chain)
     def _():
@@ -111,62 +114,96 @@
         dx, dy = (du, dv) if f == 0 else (dv, du)
         return lax.rem(x + dx, NX) * NY + lax.rem(y + dy, NY)
 
-    def gather_plan(f):
-        up, un, vp, vn = (1, 0), (3, 0), (0, 1), (0, 3)
-        own = [(up, True), (un, True), (vp, True), (vn, False)]
-        return [
-            ((0, 0), own),
-            ((1, 0), [(up, True), (vp, True), (vn, False)]),
-            ((3, 0), [(vn, True), (vp, False)]),
-            ((0, 1), [(vp, False)]),
-            ((2, 0), [(vn, True), (vp, False)]),
-            ((1, 1), [(vp, False)]),
-            ((3, 3), [(vn, False)]),
-            ((2, 3), [(vn, False)]),
-        ]
-
-    def gather_events(do):
-        plans = [gather_plan(0), gather_plan(1)]
-        n = 0
-        for e in range(len(plans[0])):
+    up, un, vp, vn = (1, 0), (3, 0), (0, 1), (0, 3)
+    relays = [
+        ((1, 0), [(up, True), (vp, True), (vn, False)]),
+        ((3, 0), [(vn, True), (vp, False)]),
+        ((0, 1), [(vp, False)]),
+        ((2, 0), [(vn, True), (vp, False)]),
+        ((1, 1), [(vp, False)]),
+        ((3, 3), [(vn, False)]),
+        ((2, 3), [(vn, False)]),
+    ]
+
+    def block_of(f, e):
+        (su, sv), _ = relays[e]
+        c = flow_cols(f, (4 - su) % 4, (4 - sv) % 4)
+        return 2 * c + f, c < 2 * row
+
+    def push(src, block, c, ssem, dev):
+        part = pl.ds(c * ROWS_C, ROWS_C)
+        remote(src.at[part], lall.at[block, part], ssem, g_rsem.at[block, c], dev).start()
+
+    def neighbour(f, send):
+        (du, dv), to_gather = send
+        return (row, flow_cols(f, du, dv) * 2 + (GATHER if to_gather else CHAIN))
+
+    def chunk_wait(block, c):
+        part = pl.ds(c * ROWS_C, ROWS_C)
+        remote(lall.at[block, part], lall.at[block, part], b_ssem, g_rsem.at[block, c], me_chain).wait_recv()
+
+    def chunks(body):
+        def one(c, _):
+            body(c)
+            return 0
+
+        lax.fori_loop(0, CHUNKS, one, 0)
+
+    @pl.when(is_gather)
+    def _():
+        own_a, own_b = 2 * chip, 2 * chip + 1
+
+        @pl.when(chip < 2 * row)
+        def _():
+            def first_a(c):
+                push(l_ref, own_a, c, g_ssem.at[0], neighbour(0, (up, True)))
+                push(l_ref, own_a, c, g_ssem.at[0], neighbour(0, (un, True)))
+
+            def first_b(c):
+                chunk_wait(own_b, c)
+                push(lall.at[own_b], own_b, c, g_ssem.at[1], neighbour(1, (up, True)))
+                push(lall.at[own_b], own_b, c, g_ssem.at[1], neighbour(1, (un, True)))
+
+            def second(c):
+                for f, src in ((0, l_ref), (1, lall.at[own_b])):
+                    push(src, own_a + f, c, g_ssem.at[f], neighbour(f, (vp, True)))
+                    push(src, own_a + f, c, g_ssem.at[f], neighbour(f, (vn, False)))
+                    push(src, own_a + f, c, g_ssem.at[f], me_chain)
+
+            chunks(first_a)
+            chunks(first_b)
+            chunks(second)
+
+        for e in range(len(relays)):
+            def relay(c):
+                for f in (0, 1):
+                    block, live = block_of(f, e)
+
+                    @pl.when(live)
+                    def _():
+                        chunk_wait(block, c)
+                        for send in relays[e][1]:
+                            push(lall.at[block], block, c, g_ssem.at[2 + 2 * e + f], neighbour(f, send))
+                        push(lall.at[block], block, c, g_ssem.at[2 + 2 * e + f], me_chain)
+
+            chunks(relay)
+
+        def sent(n, ssem):
+            remote(lall.at[pl.ds(0, n)], lall.at[pl.ds(0, n)], ssem, o_rsem, me_chain).wait_send()
+
+        @pl.when(chip < 2 * row)
+        def _():
+            sent(5, g_ssem.at[0])
+            sent(5, g_ssem.at[1])
+
+        for e in range(len(relays)):
             for f in (0, 1):
-                (su, sv), sends = plans[f][e]
-                src_chip = flow_cols(f, (4 - su) % 4, (4 - sv) % 4)
-                live = src_chip < 2 * row
-                do(f, e, src_chip, live, sends, n)
-                n += 1 + len(sends)
-
-    def copies_of(f, e, src_chip, sends, n):
-        src = l_ref if (f == GATHER and e == 0) else lall.at[src_chip, f]
-        out = []
-        for k, ((du, dv), to_gather) in enumerate(sends):
-            dest = flow_cols(f, du, dv) * 2 + (GATHER if to_gather else CHAIN)
-            out.append(remote(src, lall.at[src_chip, f], g_ssem.at[n + k], g_rsem.at[src_chip, f], (row, dest)))
-        out.append(remote(src, lall.at[src_chip, f], g_ssem.at[n + len(sends)], g_rsem.at[src_chip, f], me_chain))
-        return out
-
-    def l_piece_wait(a, f):
-        remote(lall.at[a, f], lall.at[a, f], b_ssem, g_rsem.at[a, f], me_chain).wait_recv()
-
-    @pl.when(is_gather)
-    def _():
-        def do(f, e, src_chip, live, sends, n):
-            @pl.when(live)
-            def _():
-                if not (f == GATHER and e == 0):
-                    l_piece_wait(src_chip, f)
-                for c in copies_of(f, e, src_chip, sends, n):
-                    c.start()
-
-        gather_events(do)
-
-        def done(f, e, src_chip, live, sends, n):
-            @pl.when(live)
-            def _():
-                for c in copies_of(f, e, src_chip, sends, n):
-                    c.wait_send()
-
-        gather_events(done)
+                block, live = block_of(f, e)
+
+                @pl.when(live)
+                def _():
+                    sent(len(relays[e][1]) + 1, g_ssem.at[2 + 2 * e + f])
+
         remote(s1_send, s1_send, s1_ssem, s1_rsem, me_chain).wait_send()
         remote(orecv, orecv, b_ssem, o_rsem, me_chain).wait_recv()
 
@@ -177,7 +214,7 @@
 
         @pl.when(own_live)
         def _():
-            remote(l_ref, lall.at[chip, CHAIN], b_ssem, g_rsem.at[chip, CHAIN], partner).start()
+            chunks(lambda c: push(l_ref, 2 * chip + CHAIN, c, b_ssem, partner))
 
         d = d_ref[...]
         hi, lo = split(d)
@@ -186,24 +223,25 @@
 
         width = COLS * BLK
         piv = piv_ref[...] - row * width
-        low = jnp.broadcast_to(piv & (CB - 1), (CB, ROWS * BLK))
-        hot = (lax.broadcasted_iota(jnp.int32, (CB, ROWS * BLK), 0) == low).astype(F32).astype(BF16)
-        e2[0:CB, :] = hot
-        e2[CB:, :] = hot
+        low = jnp.broadcast_to(piv & (2 * CB - 1), (2 * CB, ROWS * BLK))
+        e2[...] = (lax.broadcasted_iota(jnp.int32, (2 * CB, ROWS * BLK), 0) == low).astype(F32).astype(BF16)
 
         remote(s1_recv.at[pl.ds(0, COLS - 1)], s1_recv.at[pl.ds(0, COLS - 1)], b_ssem, s1_rsem, partner).wait_recv()
-        v = s1_recv[...].reshape(COLS * 4 * G, CB)
-        hi, lo = split(v)
-        x2[:, 0:CB] = hi
-        x2[:, CB:] = lo
+        for h in range(2):
+            v = s1_recv[:, 2 * G * h : 2 * G * h + 2 * G, :].reshape(COLS * 2 * G, CB)
+            hi, lo = split(v)
+            xhi[:, CB * h : CB * h + CB] = hi
+            xlo[:, CB * h : CB * h + CB] = lo
 
         def select(j, _):
             off = pl.multiple_of(j * BLK, BLK)
-            t = jnp.dot(x2[...], e2[:, pl.ds(off, BLK)], preferred_element_type=F32)
-            high = jnp.right_shift(piv_ref[:, pl.ds(off, BLK)] - row * width, 7)
-            rows_hi = jnp.right_shift(lax.broadcasted_iota(jnp.int32, (COLS * 4 * G, BLK), 0), 2)
+            e = e2[:, pl.ds(off, BLK)]
+            t = jnp.dot(xhi[...], e, preferred_element_type=F32)
+            t = t + jnp.dot(xlo[...], e, preferred_element_type=F32)
+            high = jnp.right_shift(piv_ref[:, pl.ds(off, BLK)] - row * width, 8)
+            rows_hi = jnp.right_shift(lax.broadcasted_iota(jnp.int32, (COLS * 2 * G, BLK), 0), 2)
             t = jnp.where(rows_hi == jnp.broadcast_to(high, rows_hi.shape), t, 0.0)
-            t = jnp.sum(t.reshape(COLS * 4 * G // 8, 8, BLK), axis=0)
+            t = jnp.sum(t.reshape(COLS, 2 * G, BLK), axis=0)
             tile = packed(t[:G] + t[G:])
 
             @pl.when(j == row)
@@ -236,9 +274,9 @@
             @pl.when(m < row)
             def _():
                 for t in range(4):
-                    l_piece_wait(2 * m + t // 2, t % 2)
+                    chunks(lambda c: chunk_wait(4 * m + t, c))
                 for t in range(4):
-                    hi, lo = split(lall[2 * m + t // 2, t % 2])
+                    hi, lo = split(lall[4 * m + t])
                     bhi[:, CB * t : CB * t + CB] = hi
                     blo[:, CB * t : CB * t + CB] = lo
 
@@ -272,7 +310,7 @@
 
         @pl.when(own_live)
         def _():
-            remote(l_ref, lall.at[chip, CHAIN], b_ssem, g_rsem.at[chip, CHAIN], partner).wait_send()
+            remote(l_ref, l_ref, b_ssem, o_rsem, partner).wait_send()
 
         remote(s1_send.at[pl.ds(0, CHIPS - 1)], s1_send.at[pl.ds(0, CHIPS - 1)], s1_ssem, s1_rsem, partner).wait_send()
         remote(s2_send.at[pl.ds(0, ROWS - 1)], s2_send.at[pl.ds(0, ROWS - 1)], s2_ssem, s2_rsem, partner).wait_send()
@@ -314,12 +352,13 @@
             pltpu.VMEM((ROWS, 8, BLK // 2), F32),
             pltpu.VMEM((ROWS, 8, BLK // 2), F32),
             pltpu.VMEM((2 * CB, ROWS * BLK), BF16),
-            pltpu.VMEM((COLS * 4 * G, 2 * CB), BF16),
+            pltpu.VMEM((COLS * 2 * G, 2 * CB), BF16),
+            pltpu.VMEM((COLS * 2 * G, 2 * CB), BF16),
             pltpu.VMEM((ROWS, 8, BLK // 2), F32),
             pltpu.VMEM((G, BLK), F32),
             pltpu.VMEM((G, BLK), F32),
             pltpu.VMEM((CHIPS, 8, CB), F32),
-            pltpu.VMEM((CHIPS, 2, BLK, CB), F32),
+            pltpu.VMEM((COLS, BLK, CB), F32),
             pltpu.VMEM((BLK, BLK), BF16),
             pltpu.VMEM((BLK, BLK), BF16),
             pltpu.VMEM((BLK, BLK), BF16),
@@ -328,8 +367,8 @@
             dma((ROWS,)),
             dma((ROWS,)),
             dma,
-            dma((48,)),
-            dma((CHIPS, 2)),
+            dma((16,)),
+            dma((COLS, CHUNKS)),
             dma,
         ],
         compiler_params=pltpu.CompilerParams(

time: 56.9 us -> 55.2 us (0.970)
  Pallas kernels: 55.4 us -> 53.3 us
    pallas_call x1, Pallas kernels: 55.4 us -> 53.3 us  [per_device(): pl.pallas_call(kernel, out_shape=jax.ShapeDtypeStruct((NRHS, CB), F32), i...]
where the time goes in v2:
time: 55.2 us; the launch traced here: 54.7 us
  Pallas kernels  53.3 us (97%)
  local copies, waits for them, and re-layouts  1.38 us (2%)
    pallas_call x1, Pallas kernels, per_device(): pl.pallas_call(kernel, out_shape=jax.ShapeDtypeStruct((NRHS, CB), F32), i...  53.3 us
    unnamed x1, local copies, waits for them, and re-layouts  1.38 us

profile of v2, /device:TPU:23, one launch (start us, length us, event | category | flops | bytes accessed | tf_op | source)
XLA Modules:
  0.0 54.7 jit_solution(767816586886721304)
XLA Ops:
  0.0 53.3 %shard_map.46 = f32[64,128]{1,0:T(8,128)} custom-call(f32[64,512]{1,0:T(8,128)} %rhs_ref.1, s32[1,4096]{1,0:T(1,128)} %bitcast.9, f32[512,128]{1,0:T(8,128)} %bitcast.7, f32[512,512]{1,0:T(8,128)} %bitcast.6), custom_call_target="tpu_custom_call" | custom-call | tf_op jit(solution)/shard_map/pallas_call | solution.py:344
  53.3 1.4 %copy.7 = f32[64,1,1,128]{3,2,1,0:T(1,128)} copy(f32[64,1,1,128]{3,2,1,0:T(1,128)} %bitcast.8) | data formatting | bytes 65536

commit v3 on v2

--- a/solution.py
+++ b/solution.py
@@ -20,6 +20,7 @@
 BF16, F32 = jnp.bfloat16, jnp.float32
 CHUNKS = 4
 ROWS_C = BLK // CHUNKS
+PART = BLK // CHIPS
 
 
 def split(v):
@@ -46,9 +47,10 @@
 
 
 def kernel(
-    rhs_ref, piv_ref, l_ref, d_ref, out_ref,
-    s1_send, s1_recv, s2_send, s2_recv, e2, xhi, xlo, ybuf, acc, pbuf, orecv, lall, bhi, blo, dhi, dlo,
+    rhs_hbm, piv_hbm, l_hbm, d_hbm, out_ref,
+    rhs_ref, piv_ref, l_ref, d_ref, in_sem, s1_send, s1_recv, s2_send, s2_recv, e2, xhi, xlo, ybuf, acc, pbuf, orecv, lall, bhi, blo, dhi, dlo,
     s1_ssem, s1_rsem, s2_ssem, s2_rsem, y_ssem, y_rsem, o_ssem, o_rsem, g_ssem, g_rsem, b_ssem,
+    sc_ssem, u_rsem, w_rsem, c_rsem, un_ssem,
 ):
     row = lax.axis_index("row")
     col = lax.axis_index("col")
@@ -56,6 +58,8 @@
     x, y = chip // NY, chip % NY
     is_chain = core == CHAIN
     is_gather = core == GATHER
+    scattered = (row > 0) & (row <= 3)
+    relaying = row > 3
 
     def chain_col(c):
         return 2 * c + CHAIN
@@ -81,13 +85,36 @@
     def _():
         lax.fori_loop(1, ROWS, greet_z, 0)
 
+    load_rhs = pltpu.make_async_copy(rhs_hbm, rhs_ref, in_sem.at[0])
+    load_l = pltpu.make_async_copy(l_hbm, l_ref, in_sem.at[1])
+    load_piv = pltpu.make_async_copy(piv_hbm, piv_ref, in_sem.at[2])
+    load_d = pltpu.make_async_copy(d_hbm, d_ref, in_sem.at[3])
+    load_rhs.start()
+    load_l.start()
+
+    @pl.when(is_chain)
+    def _():
+        load_piv.start()
+        load_d.start()
+
+    load_rhs.wait()
+
     for c in range(CHIPS):
         for q in range(4):
             at = 2 * G * (q % 2) + G * (q // 2)
             s1_send[c, at : at + G, :] = rhs_ref[G * c : G * c + G, CB * q : CB * q + CB]
 
+    load_l.wait()
+
+    @pl.when(is_gather & scattered)
+    def _():
+        part = pl.ds(pl.multiple_of(chip * PART, PART), PART)
+        lall[col, part] = l_ref[part]
+
     @pl.when(is_chain)
     def _():
+        load_piv.wait()
+        load_d.wait()
         pl.semaphore_wait(barrier, COLS - 1 + ROWS - 1)
 
     @pl.when(is_gather)
@@ -110,33 +137,41 @@
 
     me_chain = (row, chain_col(chip))
 
-    def flow_cols(f, du, dv):
+
+    def flow_chip(f, du, dv):
         dx, dy = (du, dv) if f == 0 else (dv, du)
         return lax.rem(x + dx, NX) * NY + lax.rem(y + dy, NY)
 
-    up, un, vp, vn = (1, 0), (3, 0), (0, 1), (0, 3)
-    relays = [
-        ((1, 0), [(up, True), (vp, True), (vn, False)]),
-        ((3, 0), [(vn, True), (vp, False)]),
-        ((0, 1), [(vp, False)]),
-        ((2, 0), [(vn, True), (vp, False)]),
-        ((1, 1), [(vp, False)]),
-        ((3, 3), [(vn, False)]),
-        ((2, 3), [(vn, False)]),
-    ]
-
-    def block_of(f, e):
-        (su, sv), _ = relays[e]
-        c = flow_cols(f, (4 - su) % 4, (4 - sv) % 4)
+    def place(f):
+        return (x, y) if f == 0 else (y, x)
+
+    by_second_only = row == 4
+
+    def upward(f, du, dv=None):
+        u, v = place(f)
+        first = lax.rem(u - du + NX, NX)
+        if dv is None:
+            return lax.rem(first, 2) == 1
+        second = lax.rem(v - dv + NY, NY)
+        return lax.rem(second + jnp.where(by_second_only, 0, first), 2) == 1
+
+    def block_of(f, du, dv):
+        c = flow_chip(f, (4 - du) % 4, (4 - dv) % 4)
         return 2 * c + f, c < 2 * row
 
     def push(src, block, c, ssem, dev):
         part = pl.ds(c * ROWS_C, ROWS_C)
         remote(src.at[part], lall.at[block, part], ssem, g_rsem.at[block, c], dev).start()
 
-    def neighbour(f, send):
-        (du, dv), to_gather = send
-        return (row, flow_cols(f, du, dv) * 2 + (GATHER if to_gather else CHAIN))
+    def neighbour(f, du, dv, relayed=True):
+        role = jnp.where(relayed, GATHER, CHAIN) if not isinstance(relayed, bool) else (GATHER if relayed else CHAIN)
+        return (row, flow_chip(f, du, dv) * 2 + role)
+
+    def spread(f, du, src, block, c, ssem):
+        plus = upward(f, du, 0)
+        push(src, block, c, ssem, neighbour(f, 0, 1, plus))
+        push(src, block, c, ssem, neighbour(f, 0, 3, jnp.logical_not(plus)))
+        push(src, block, c, ssem, me_chain)
 
     def chunk_wait(block, c):
         part = pl.ds(c * ROWS_C, ROWS_C)
@@ -149,61 +184,186 @@
 
         lax.fori_loop(0, CHUNKS, one, 0)
 
-    @pl.when(is_gather)
+    def scatter(ssem):
+        m, f = jnp.minimum(chip // 2, 2), lax.rem(chip, 2)
+
+        def one(i, _):
+            c = lax.rem(chip + i, CHIPS)
+            part = pl.ds(pl.multiple_of(c * PART, PART), PART)
+            remote(l_ref.at[part], lall.at[col, part], ssem, u_rsem.at[m, f], (row, 2 * c + GATHER)).start()
+            return 0
+
+        return one
+
+    def unit(c, f, m):
+        return lall.at[pl.ds(4 * m + 2 * f, 2), pl.ds(pl.multiple_of(c * PART, PART), PART)]
+
+    def unit_of(f, du):
+        return flow_chip(f, (4 - du) % 4, 0)
+
+    def unit_send(c, f, m, rsem, dev):
+        remote(unit(c, f, m), unit(c, f, m), un_ssem.at[m], rsem, dev).start()
+
+    def unit_spread(c, f, m):
+        for dv in (1, 3, 2):
+            unit_send(c, f, m, c_rsem.at[m], (row, chain_col(flow_chip(f, 0, dv))))
+        unit_send(c, f, m, c_rsem.at[m], me_chain)
+
+    @pl.when(is_gather & scattered)
+    def _():
+        @pl.when(chip < 2 * row)
+        def _():
+            lax.fori_loop(1, CHIPS, scatter(sc_ssem), 0)
+
+        def own_units(m, _):
+            for f in (0, 1):
+                ref = lall.at[pl.ds(4 * m + 2 * f, 2), pl.ds(0, PART)]
+                one = lall.at[pl.ds(4 * m + 2 * f, 1), pl.ds(0, PART)]
+
+                @pl.when(chip == 2 * m + f)
+                def _():
+                    remote(one, one, b_ssem, u_rsem.at[m, f], me_chain).wait_recv()
+
+                @pl.when(chip != 2 * m + f)
+                def _():
+                    remote(ref, ref, b_ssem, u_rsem.at[m, f], me_chain).wait_recv()
+
+                for du in (1, 3, 2):
+                    unit_send(chip, f, m, w_rsem.at[du, m, f], (row, 2 * flow_chip(f, du, 0) + GATHER))
+                unit_spread(chip, f, m)
+            return 0
+
+        def relay_units(m, _):
+            for du in (1, 3, 2):
+                for f in (0, 1):
+                    c = unit_of(f, du)
+                    remote(unit(c, f, m), unit(c, f, m), b_ssem, w_rsem.at[du, m, f], me_chain).wait_recv()
+                    unit_spread(c, f, m)
+            return 0
+
+        def units_sent(m, _):
+            ref = lall.at[pl.ds(0, 19), pl.ds(0, 4 * PART)]
+            remote(ref, ref, un_ssem.at[m], o_rsem, me_chain).wait_send()
+            return 0
+
+        lax.fori_loop(0, row, own_units, 0)
+        lax.fori_loop(0, row, relay_units, 0)
+        lax.fori_loop(0, row, units_sent, 0)
+
+        @pl.when(chip < 2 * row)
+        def _():
+            ref = l_ref.at[pl.ds(0, BLK - PART)]
+            remote(ref, ref, sc_ssem, o_rsem, me_chain).wait_send()
+
+    @pl.when(is_gather & relaying)
     def _():
         own_a, own_b = 2 * chip, 2 * chip + 1
 
         @pl.when(chip < 2 * row)
         def _():
             def first_a(c):
-                push(l_ref, own_a, c, g_ssem.at[0], neighbour(0, (up, True)))
-                push(l_ref, own_a, c, g_ssem.at[0], neighbour(0, (un, True)))
+                push(l_ref, own_a, c, g_ssem.at[0], neighbour(0, 1, 0))
+                push(l_ref, own_a, c, g_ssem.at[0], neighbour(0, 3, 0))
 
             def first_b(c):
                 chunk_wait(own_b, c)
-                push(lall.at[own_b], own_b, c, g_ssem.at[1], neighbour(1, (up, True)))
-                push(lall.at[own_b], own_b, c, g_ssem.at[1], neighbour(1, (un, True)))
+                push(lall.at[own_b], own_b, c, g_ssem.at[1], neighbour(1, 1, 0))
+                push(lall.at[own_b], own_b, c, g_ssem.at[1], neighbour(1, 3, 0))
 
             def second(c):
-                for f, src in ((0, l_ref), (1, lall.at[own_b])):
-                    push(src, own_a + f, c, g_ssem.at[f], neighbour(f, (vp, True)))
-                    push(src, own_a + f, c, g_ssem.at[f], neighbour(f, (vn, False)))
-                    push(src, own_a + f, c, g_ssem.at[f], me_chain)
+                spread(0, 0, l_ref, own_a, c, g_ssem.at[0])
+                spread(1, 0, lall.at[own_b], own_b, c, g_ssem.at[1])
 
             chunks(first_a)
             chunks(first_b)
             chunks(second)
 
-        for e in range(len(relays)):
-            def relay(c):
+        def on_first(du, c, f):
+            block, live = block_of(f, du, 0)
+
+            @pl.when(live)
+            def _():
+                chunk_wait(block, c)
+                if du != 2:
+                    onward = upward(f, du) if du == 1 else jnp.logical_not(upward(f, du))
+
+                    @pl.when(onward)
+                    def _():
+                        push(lall.at[block], block, c, g_ssem.at[4 * du + 2 + f], neighbour(f, du, 0))
+
+                spread(f, du, lall.at[block], block, c, g_ssem.at[4 * du + f])
+
+        def second_state(f, du, dv):
+            block, live = block_of(f, du, dv)
+            onward = upward(f, du, dv) if dv == 1 else jnp.logical_not(upward(f, du, dv))
+            return block, live & onward, 16 + 4 * du + (dv - 1) + f
+
+        def on_second(du, dv, c, f):
+            block, go, at = second_state(f, du, dv)
+
+            @pl.when(go)
+            def _():
+                chunk_wait(block, c)
+                push(lall.at[block], block, c, g_ssem.at[at], neighbour(f, 0, dv, False))
+                push(lall.at[block], block, c, g_ssem.at[at], me_chain)
+
+        def first_both(c):
+            for f in (0, 1):
+                on_first(1, c, f)
+                on_first(3, c, f)
+
+        def second_of(*dus):
+            def body(c):
                 for f in (0, 1):
-                    block, live = block_of(f, e)
-
-                    @pl.when(live)
-                    def _():
-                        chunk_wait(block, c)
-                        for send in relays[e][1]:
-                            push(lall.at[block], block, c, g_ssem.at[2 + 2 * e + f], neighbour(f, send))
-                        push(lall.at[block], block, c, g_ssem.at[2 + 2 * e + f], me_chain)
-
-            chunks(relay)
+                    for du in dus:
+                        on_second(du, 1, c, f)
+                        on_second(du, 3, c, f)
+
+            return body
+
+        def first_far(c):
+            for f in (0, 1):
+                on_first(2, c, f)
+
+        chunks(first_both)
+        chunks(second_of(0))
+        chunks(first_far)
+        chunks(second_of(1, 3))
+        chunks(second_of(2))
 
         def sent(n, ssem):
             remote(lall.at[pl.ds(0, n)], lall.at[pl.ds(0, n)], ssem, o_rsem, me_chain).wait_send()
 
-        @pl.when(chip < 2 * row)
-        def _():
-            sent(5, g_ssem.at[0])
-            sent(5, g_ssem.at[1])
-
-        for e in range(len(relays)):
-            for f in (0, 1):
-                block, live = block_of(f, e)
+        for f in (0, 1):
+
+            @pl.when(chip < 2 * row)
+            def _():
+                sent(5, g_ssem.at[f])
+
+            for du in (1, 2, 3):
+                block, live = block_of(f, du, 0)
 
                 @pl.when(live)
                 def _():
-                    sent(len(relays[e][1]) + 1, g_ssem.at[2 + 2 * e + f])
-
+                    sent(3, g_ssem.at[4 * du + f])
+
+                if du != 2:
+                    onward = upward(f, du) if du == 1 else jnp.logical_not(upward(f, du))
+
+                    @pl.when(live & onward)
+                    def _():
+                        sent(1, g_ssem.at[4 * du + 2 + f])
+
+            for du in range(4):
+                for dv in (1, 3):
+                    _, go, at = second_state(f, du, dv)
+
+                    @pl.when(go)
+                    def _():
+                        sent(2, g_ssem.at[at])
+
+    @pl.when(is_gather)
+    def _():
         remote(s1_send, s1_send, s1_ssem, s1_rsem, me_chain).wait_send()
         remote(orecv, orecv, b_ssem, o_rsem, me_chain).wait_recv()
 
@@ -212,9 +372,13 @@
         partner = (row, 2 * chip + GATHER)
         own_live = chip < 2 * row
 
-        @pl.when(own_live)
+        @pl.when(own_live & relaying)
         def _():
             chunks(lambda c: push(l_ref, 2 * chip + CHAIN, c, b_ssem, partner))
+
+        @pl.when(own_live & scattered)
+        def _():
+            lax.fori_loop(0, CHIPS, scatter(b_ssem), 0)
 
         d = d_ref[...]
         hi, lo = split(d)
@@ -273,8 +437,16 @@
         def step(m, _):
             @pl.when(m < row)
             def _():
-                for t in range(4):
-                    chunks(lambda c: chunk_wait(4 * m + t, c))
+                @pl.when(relaying)
+                def _():
+                    for t in range(4):
+                        chunks(lambda c: chunk_wait(4 * m + t, c))
+
+                @pl.when(scattered)
+                def _():
+                    four = lall.at[pl.ds(4 * m, 4)]
+                    remote(four, four, b_ssem, c_rsem.at[m], partner).wait_recv()
+
                 for t in range(4):
                     hi, lo = split(lall[4 * m + t])
                     bhi[:, CB * t : CB * t + CB] = hi
@@ -339,14 +511,19 @@
 
 
 def per_device(rhs, pivots, factor, diag_inv):
-    vmem = pl.BlockSpec(memory_space=pltpu.VMEM)
+    hbm = pl.BlockSpec(memory_space=pltpu.HBM)
     dma = pltpu.SemaphoreType.DMA
     out = pl.pallas_call(
         kernel,
         out_shape=jax.ShapeDtypeStruct((NRHS, CB), F32),
-        in_specs=[vmem] * 4,
-        out_specs=vmem,
+        in_specs=[hbm] * 4,
+        out_specs=pl.BlockSpec(memory_space=pltpu.VMEM),
         scratch_shapes=[
+            pltpu.VMEM((NRHS, BLK), F32),
+            pltpu.VMEM((1, ROWS * BLK), jnp.int32),
+            pltpu.VMEM((BLK, CB), F32),
+            pltpu.VMEM((BLK, BLK), F32),
+            dma((4,)),
             pltpu.VMEM((CHIPS, 4 * G, CB), F32),
             pltpu.VMEM((COLS, 4 * G, CB), F32),
             pltpu.VMEM((ROWS, 8, BLK // 2), F32),
@@ -367,9 +544,14 @@
             dma((ROWS,)),
             dma((ROWS,)),
             dma,
-            dma((16,)),
+            dma((32,)),
             dma((COLS, CHUNKS)),
             dma,
+            dma,
+            dma((3, 2)),
+            dma((4, 3, 2)),
+            dma((3,)),
+            dma((3,)),
         ],
         compiler_params=pltpu.CompilerParams(
             collective_id=0, has_side_effects=True, vmem_limit_bytes=56 * 1024 * 1024

time: 55.2 us -> 52.2 us (0.946)
  Pallas kernels: 53.3 us -> 50.7 us
    pallas_call x1, Pallas kernels: 53.3 us -> 50.7 us  [per_device(): pl.pallas_call(kernel, out_shape=jax.ShapeDtypeStruct((NRHS, CB), F32), i...]
where the time goes in v3:
time: 52.2 us; the launch traced here: 52.1 us
  Pallas kernels  50.7 us (97%)
  local copies, waits for them, and re-layouts  1.38 us (3%)
    pallas_call x1, Pallas kernels, per_device(): pl.pallas_call(kernel, out_shape=jax.ShapeDtypeStruct((NRHS, CB), F32), i...  50.7 us
    unnamed x1, local copies, waits for them, and re-layouts  1.38 us

profile of v3, /device:TPU:23, one launch (start us, length us, event | category | flops | bytes accessed | tf_op | source)
XLA Modules:
  0.0 52.1 jit_solution(17983491129213748694)
XLA Ops:
  0.0 50.7 %shard_map.46 = f32[64,128]{1,0:T(8,128)} custom-call(f32[64,512]{1,0:T(8,128)} %rhs_hbm.1, s32[1,4096]{1,0:T(1,128)} %bitcast.9, f32[512,128]{1,0:T(8,128)} %bitcast.7, f32[512,512]{1,0:T(8,128)} %bitcast.6), custom_call_target="tpu_custom_call" | custom-call | tf_op jit(solution)/shard_map/pallas_call | solution.py:516
  50.7 1.4 %copy.7 = f32[64,1,1,128]{3,2,1,0:T(1,128)} copy(f32[64,1,1,128]{3,2,1,0:T(1,128)} %bitcast.8) | data formatting | bytes 65536

commit v4 on v3

--- a/solution.py
+++ b/solution.py
@@ -121,6 +121,27 @@
     def _():
         pl.semaphore_wait(barrier, COLS - 1)
 
+    def scatter(ssem):
+        m, f = jnp.minimum(chip // 2, 2), lax.rem(chip, 2)
+
+        def one(i, _):
+            c = lax.rem(chip + i, CHIPS)
+            part = pl.ds(pl.multiple_of(c * PART, PART), PART)
+            remote(l_ref.at[part], lall.at[col, part], ssem, u_rsem.at[m, f], (row, 2 * c + GATHER)).start()
+            return 0
+
+        return one
+
+    own_live = chip < 2 * row
+
+    @pl.when(own_live & scattered & is_gather)
+    def _():
+        lax.fori_loop(1, CHIPS, scatter(sc_ssem), 0)
+
+    @pl.when(own_live & scattered & is_chain)
+    def _():
+        lax.fori_loop(0, CHIPS, scatter(b_ssem), 0)
+
     def send_s1(i, _):
         c = lax.rem(chip + i, CHIPS)
         remote(s1_send.at[c], s1_recv.at[col], s1_ssem, s1_rsem, (row, chain_col(c))).start()
@@ -145,15 +166,15 @@
     def place(f):
         return (x, y) if f == 0 else (y, x)
 
-    by_second_only = row == 4
-
-    def upward(f, du, dv=None):
+    by_chunk = row > 4
+
+    def upward(f, c, du, dv=None):
         u, v = place(f)
         first = lax.rem(u - du + NX, NX)
         if dv is None:
-            return lax.rem(first, 2) == 1
+            return lax.rem(first + jnp.where(by_chunk, c, 0), 2) == 1
         second = lax.rem(v - dv + NY, NY)
-        return lax.rem(second + jnp.where(by_second_only, 0, first), 2) == 1
+        return lax.rem(second + jnp.where(by_chunk, c + first, 0), 2) == 1
 
     def block_of(f, du, dv):
         c = flow_chip(f, (4 - du) % 4, (4 - dv) % 4)
@@ -168,7 +189,7 @@
         return (row, flow_chip(f, du, dv) * 2 + role)
 
     def spread(f, du, src, block, c, ssem):
-        plus = upward(f, du, 0)
+        plus = upward(f, c, du, 0)
         push(src, block, c, ssem, neighbour(f, 0, 1, plus))
         push(src, block, c, ssem, neighbour(f, 0, 3, jnp.logical_not(plus)))
         push(src, block, c, ssem, me_chain)
@@ -183,17 +204,6 @@
             return 0
 
         lax.fori_loop(0, CHUNKS, one, 0)
-
-    def scatter(ssem):
-        m, f = jnp.minimum(chip // 2, 2), lax.rem(chip, 2)
-
-        def one(i, _):
-            c = lax.rem(chip + i, CHIPS)
-            part = pl.ds(pl.multiple_of(c * PART, PART), PART)
-            remote(l_ref.at[part], lall.at[col, part], ssem, u_rsem.at[m, f], (row, 2 * c + GATHER)).start()
-            return 0
-
-        return one
 
     def unit(c, f, m):
         return lall.at[pl.ds(4 * m + 2 * f, 2), pl.ds(pl.multiple_of(c * PART, PART), PART)]
@@ -211,10 +221,6 @@
 
     @pl.when(is_gather & scattered)
     def _():
-        @pl.when(chip < 2 * row)
-        def _():
-            lax.fori_loop(1, CHIPS, scatter(sc_ssem), 0)
-
         def own_units(m, _):
             for f in (0, 1):
                 ref = lall.at[pl.ds(4 * m + 2 * f, 2), pl.ds(0, PART)]
@@ -285,7 +291,7 @@
             def _():
                 chunk_wait(block, c)
                 if du != 2:
-                    onward = upward(f, du) if du == 1 else jnp.logical_not(upward(f, du))
+                    onward = upward(f, c, du) if du == 1 else jnp.logical_not(upward(f, c, du))
 
                     @pl.when(onward)
                     def _():
@@ -293,13 +299,13 @@
 
                 spread(f, du, lall.at[block], block, c, g_ssem.at[4 * du + f])
 
-        def second_state(f, du, dv):
+        def second_state(f, c, du, dv):
             block, live = block_of(f, du, dv)
-            onward = upward(f, du, dv) if dv == 1 else jnp.logical_not(upward(f, du, dv))
+            onward = upward(f, c, du, dv) if dv == 1 else jnp.logical_not(upward(f, c, du, dv))
             return block, live & onward, 16 + 4 * du + (dv - 1) + f
 
         def on_second(du, dv, c, f):
-            block, go, at = second_state(f, du, dv)
+            block, go, at = second_state(f, c, du, dv)
 
             @pl.when(go)
             def _():
@@ -334,6 +340,16 @@
         def sent(n, ssem):
             remote(lall.at[pl.ds(0, n)], lall.at[pl.ds(0, n)], ssem, o_rsem, me_chain).wait_send()
 
+        def some_sent(live, go, n, ssem):
+            @pl.when(live & by_chunk)
+            def _():
+                ref = lall.at[pl.ds(0, n), pl.ds(0, BLK // 2)]
+                remote(ref, ref, ssem, o_rsem, me_chain).wait_send()
+
+            @pl.when(live & go & jnp.logical_not(by_chunk))
+            def _():
+                sent(n, ssem)
+
         for f in (0, 1):
 
             @pl.when(chip < 2 * row)
@@ -348,19 +364,14 @@
                     sent(3, g_ssem.at[4 * du + f])
 
                 if du != 2:
-                    onward = upward(f, du) if du == 1 else jnp.logical_not(upward(f, du))
-
-                    @pl.when(live & onward)
-                    def _():
-                        sent(1, g_ssem.at[4 * du + 2 + f])
+                    onward = upward(f, 0, du) if du == 1 else jnp.logical_not(upward(f, 0, du))
+                    some_sent(live, onward, 1, g_ssem.at[4 * du + 2 + f])
 
             for du in range(4):
                 for dv in (1, 3):
-                    _, go, at = second_state(f, du, dv)
-
-                    @pl.when(go)
-                    def _():
-                        sent(2, g_ssem.at[at])
+                    live = block_of(f, du, dv)[1]
+                    _, go, at = second_state(f, 0, du, dv)
+                    some_sent(live, go, 2, g_ssem.at[at])
 
     @pl.when(is_gather)
     def _():
@@ -370,15 +381,9 @@
     @pl.when(is_chain)
     def _():
         partner = (row, 2 * chip + GATHER)
-        own_live = chip < 2 * row
-
         @pl.when(own_live & relaying)
         def _():
             chunks(lambda c: push(l_ref, 2 * chip + CHAIN, c, b_ssem, partner))
-
-        @pl.when(own_live & scattered)
-        def _():
-            lax.fori_loop(0, CHIPS, scatter(b_ssem), 0)
 
         d = d_ref[...]
         hi, lo = split(d)
@@ -515,7 +520,7 @@
     dma = pltpu.SemaphoreType.DMA
     out = pl.pallas_call(
         kernel,
-        out_shape=jax.ShapeDtypeStruct((NRHS, CB), F32),
+        out_shape=pltpu.VMEM((NRHS, CB), F32),
         in_specs=[hbm] * 4,
         out_specs=pl.BlockSpec(memory_space=pltpu.VMEM),
         scratch_shapes=[
@@ -554,7 +559,7 @@
             dma((3,)),
         ],
         compiler_params=pltpu.CompilerParams(
-            collective_id=0, has_side_effects=True, vmem_limit_bytes=56 * 1024 * 1024
+            collective_id=0, has_side_effects=True, vmem_limit_bytes=55200 * 1024
         ),
     )(
         rhs,

time: 52.2 us -> 49.1 us (0.941)
  Pallas kernels: 50.7 us -> 48 us
  local copies, waits for them, and re-layouts: 1.38 us -> 0.62 us
    pallas_call x1, Pallas kernels: 50.7 us -> 48 us  [per_device(): pl.pallas_call(kernel, out_shape=pltpu.VMEM((NRHS, CB), F32), in_specs=[h...]
    unnamed x1, local copies, waits for them, and re-layouts: 1.38 us -> 0.62 us
where the time goes in v4:
time: 49.1 us; the launch traced here: 48.7 us
  Pallas kernels  48 us (98%)
  local copies, waits for them, and re-layouts  0.62 us (1%)
    pallas_call x1, Pallas kernels, per_device(): pl.pallas_call(kernel, out_shape=pltpu.VMEM((NRHS, CB), F32), in_specs=[h...  48 us

profile of v4, /device:TPU:23, one launch (start us, length us, event | category | flops | bytes accessed | tf_op | source)
XLA Modules:
  0.0 48.7 jit_solution(2356849939454104828)
XLA Ops:
  0.0 48.0 %shard_map.46 = f32[64,128]{1,0:T(8,128)S(1)} custom-call(f32[64,512]{1,0:T(8,128)} %rhs_hbm.1, s32[1,4096]{1,0:T(1,128)} %bitcast.9, f32[512,128]{1,0:T(8,128)} %bitcast.8, f32[512,512]{1,0:T(8,128)} %bitcast.7), custom_call_target="tpu_custom_call" | custom-call | tf_op jit(solution)/shard_map/pallas_call | solution.py:521
  48.0 0.6 %copy.7 = f32[64,1,1,128]{3,2,1,0:T(1,128)} copy(f32[64,1,1,128]{3,2,1,0:T(1,128)S(1)} %bitcast.6) | data formatting | bytes 65536

commit v5 on v4

--- a/solution.py
+++ b/solution.py
@@ -19,8 +19,8 @@
 CHAIN, GATHER = 1, 0
 BF16, F32 = jnp.bfloat16, jnp.float32
 CHUNKS = 4
-ROWS_C = BLK // CHUNKS
-PART = BLK // CHIPS
+ROWS_C = CB // CHUNKS
+PART = CB // CHIPS
 
 
 def split(v):
@@ -37,18 +37,17 @@
     return jnp.concatenate([v[:G], v[G:]], axis=1)
 
 
-def times_t(v, hi_ref, lo_ref):
+def times(v, hi_ref, lo_ref):
     hi, lo = split(v)
     lhs = jnp.concatenate([hi.astype(F32), lo.astype(F32)], axis=0).astype(BF16)
-    dims = (((1,), (1,)), ((), ()))
-    o = lax.dot_general(lhs, hi_ref[...], dims, preferred_element_type=F32)
-    o = o + lax.dot_general(lhs, lo_ref[...], dims, preferred_element_type=F32)
+    o = jnp.dot(lhs, hi_ref[...], preferred_element_type=F32)
+    o = o + jnp.dot(lhs, lo_ref[...], preferred_element_type=F32)
     return o[:G] + o[G:]
 
 
 def kernel(
     rhs_hbm, piv_hbm, l_hbm, d_hbm, out_ref,
-    rhs_ref, piv_ref, l_ref, d_ref, in_sem, s1_send, s1_recv, s2_send, s2_recv, e2, xhi, xlo, ybuf, acc, pbuf, orecv, lall, bhi, blo, dhi, dlo,
+    rhs_ref, piv_ref, l_in, l_ref, d_ref, in_sem, s1_send, s1_recv, s2_send, s2_recv, e2, xhi, xlo, ybuf, acc, pbuf, orecv, lall, bhi, blo, dhi, dlo,
     s1_ssem, s1_rsem, s2_ssem, s2_rsem, y_ssem, y_rsem, o_ssem, o_rsem, g_ssem, g_rsem, b_ssem,
     sc_ssem, u_rsem, w_rsem, c_rsem, un_ssem,
 ):
@@ -86,7 +85,7 @@
         lax.fori_loop(1, ROWS, greet_z, 0)
 
     load_rhs = pltpu.make_async_copy(rhs_hbm, rhs_ref, in_sem.at[0])
-    load_l = pltpu.make_async_copy(l_hbm, l_ref, in_sem.at[1])
+    load_l = pltpu.make_async_copy(l_hbm, l_in, in_sem.at[1])
     load_piv = pltpu.make_async_copy(piv_hbm, piv_ref, in_sem.at[2])
     load_d = pltpu.make_async_copy(d_hbm, d_ref, in_sem.at[3])
     load_rhs.start()
@@ -105,6 +104,7 @@
             s1_send[c, at : at + G, :] = rhs_ref[G * c : G * c + G, CB * q : CB * q + CB]
 
     load_l.wait()
+    l_ref[...] = l_in[...].T
 
     @pl.when(is_gather & scattered)
     def _():
@@ -258,7 +258,7 @@
 
         @pl.when(chip < 2 * row)
         def _():
-            ref = l_ref.at[pl.ds(0, BLK - PART)]
+            ref = l_ref.at[pl.ds(0, CB - PART)]
             remote(ref, ref, sc_ssem, o_rsem, me_chain).wait_send()
 
     @pl.when(is_gather & relaying)
@@ -343,7 +343,7 @@
         def some_sent(live, go, n, ssem):
             @pl.when(live & by_chunk)
             def _():
-                ref = lall.at[pl.ds(0, n), pl.ds(0, BLK // 2)]
+                ref = lall.at[pl.ds(0, n), pl.ds(0, CB // 2)]
                 remote(ref, ref, ssem, o_rsem, me_chain).wait_send()
 
             @pl.when(live & go & jnp.logical_not(by_chunk))
@@ -385,7 +385,7 @@
         def _():
             chunks(lambda c: push(l_ref, 2 * chip + CHAIN, c, b_ssem, partner))
 
-        d = d_ref[...]
+        d = d_ref[...].T
         hi, lo = split(d)
         dhi[...] = hi
         dlo[...] = lo
@@ -430,7 +430,7 @@
         acc[...] = jnp.zeros_like(acc)
 
         def finish():
-            fresh = times_t(pbuf[...] - acc[...], dhi, dlo)
+            fresh = times(pbuf[...] - acc[...], dhi, dlo)
             ybuf[row] = packed(fresh)
             for i in range(1, ROWS):
                 remote(ybuf.at[row], ybuf.at[row], y_ssem, y_rsem.at[row], (lax.rem(row + i, ROWS), col)).start()
@@ -454,8 +454,8 @@
 
                 for t in range(4):
                     hi, lo = split(lall[4 * m + t])
-                    bhi[:, CB * t : CB * t + CB] = hi
-                    blo[:, CB * t : CB * t + CB] = lo
+                    bhi[CB * t : CB * t + CB, :] = hi
+                    blo[CB * t : CB * t + CB, :] = lo
 
             @pl.when(m != row)
             def _():
@@ -463,7 +463,7 @@
 
             @pl.when(m < row)
             def _():
-                acc[...] += times_t(unpacked(ybuf[m]), bhi, blo)
+                acc[...] += times(unpacked(ybuf[m]), bhi, blo)
 
             @pl.when(m + 1 == row)
             def _():
@@ -527,6 +527,7 @@
             pltpu.VMEM((NRHS, BLK), F32),
             pltpu.VMEM((1, ROWS * BLK), jnp.int32),
             pltpu.VMEM((BLK, CB), F32),
+            pltpu.VMEM((CB, BLK), F32),
             pltpu.VMEM((BLK, BLK), F32),
             dma((4,)),
             pltpu.VMEM((CHIPS, 4 * G, CB), F32),
@@ -540,7 +541,7 @@
             pltpu.VMEM((G, BLK), F32),
             pltpu.VMEM((G, BLK), F32),
             pltpu.VMEM((CHIPS, 8, CB), F32),
-            pltpu.VMEM((COLS, BLK, CB), F32),
+            pltpu.VMEM((COLS, CB, BLK), F32),
             pltpu.VMEM((BLK, BLK), BF16),
             pltpu.VMEM((BLK, BLK), BF16),
             pltpu.VMEM((BLK, BLK), BF16),

time: 49.1 us -> 48 us (0.978)
  Pallas kernels: 48 us -> 46.8 us
    pallas_call x1, Pallas kernels: 48 us -> 46.8 us  [per_device(): pl.pallas_call(kernel, out_shape=pltpu.VMEM((NRHS, CB), F32), in_specs=[h...]
where the time goes in v5:
time: 48 us; the launch traced here: 47.5 us
  Pallas kernels  46.8 us (98%)
  local copies, waits for them, and re-layouts  0.62 us (1%)
    pallas_call x1, Pallas kernels, per_device(): pl.pallas_call(kernel, out_shape=pltpu.VMEM((NRHS, CB), F32), in_specs=[h...  46.8 us

profile of v5, /device:TPU:23, one launch (start us, length us, event | category | flops | bytes accessed | tf_op | source)
XLA Modules:
  0.0 47.5 jit_solution(592512744728576557)
XLA Ops:
  0.0 46.8 %shard_map.46 = f32[64,128]{1,0:T(8,128)S(1)} custom-call(f32[64,512]{1,0:T(8,128)} %rhs_hbm.1, s32[1,4096]{1,0:T(1,128)} %bitcast.9, f32[512,128]{1,0:T(8,128)} %bitcast.8, f32[512,512]{1,0:T(8,128)} %bitcast.7), custom_call_target="tpu_custom_call" | custom-call | tf_op jit(solution)/shard_map/pallas_call | solution.py:521
  46.9 0.6 %copy.7 = f32[64,1,1,128]{3,2,1,0:T(1,128)} copy(f32[64,1,1,128]{3,2,1,0:T(1,128)S(1)} %bitcast.6) | data formatting | bytes 65536

commit v6 on v5

--- a/solution.py
+++ b/solution.py
@@ -166,15 +166,20 @@
     def place(f):
         return (x, y) if f == 0 else (y, x)
 
-    by_chunk = row > 4
-
     def upward(f, c, du, dv=None):
         u, v = place(f)
         first = lax.rem(u - du + NX, NX)
         if dv is None:
-            return lax.rem(first + jnp.where(by_chunk, c, 0), 2) == 1
-        second = lax.rem(v - dv + NY, NY)
-        return lax.rem(second + jnp.where(by_chunk, c + first, 0), 2) == 1
+            odd = lax.rem(first + c, 2) == 1
+            along_x, at_x = f == 0, first
+        else:
+            second = lax.rem(v - dv + NY, NY)
+            odd = lax.rem(first + second + c, 2) == 1
+            along_x, at_x = f == 1, second
+        if not along_x:
+            return odd
+        uneven = (at_x == 2) | ((at_x == 1) & ((row == 4) | (c != 0)))
+        return ((row >= 6) & odd) | ((row < 6) & uneven)
 
     def block_of(f, du, dv):
         c = flow_chip(f, (4 - du) % 4, (4 - dv) % 4)
@@ -215,9 +220,9 @@
         remote(unit(c, f, m), unit(c, f, m), un_ssem.at[m], rsem, dev).start()
 
     def unit_spread(c, f, m):
-        for dv in (1, 3, 2):
+        unit_send(c, f, m, c_rsem.at[m], me_chain)
+        for dv in (2, 3, 1):
             unit_send(c, f, m, c_rsem.at[m], (row, chain_col(flow_chip(f, 0, dv))))
-        unit_send(c, f, m, c_rsem.at[m], me_chain)
 
     @pl.when(is_gather & scattered)
     def _():
@@ -234,8 +239,12 @@
                 def _():
                     remote(ref, ref, b_ssem, u_rsem.at[m, f], me_chain).wait_recv()
 
-                for du in (1, 3, 2):
+                for du in (2, 1, 3):
                     unit_send(chip, f, m, w_rsem.at[du, m, f], (row, 2 * flow_chip(f, du, 0) + GATHER))
+            return 0
+
+        def own_spread(m, _):
+            for f in (0, 1):
                 unit_spread(chip, f, m)
             return 0
 
@@ -253,6 +262,7 @@
             return 0
 
         lax.fori_loop(0, row, own_units, 0)
+        lax.fori_loop(0, row, own_spread, 0)
         lax.fori_loop(0, row, relay_units, 0)
         lax.fori_loop(0, row, units_sent, 0)
 
@@ -276,38 +286,50 @@
                 push(lall.at[own_b], own_b, c, g_ssem.at[1], neighbour(1, 1, 0))
                 push(lall.at[own_b], own_b, c, g_ssem.at[1], neighbour(1, 3, 0))
 
-            def second(c):
+            chunks(first_a)
+            chunks(first_b)
+
+        def first_onward(f, c, du):
+            return upward(f, c, du) if du == 1 else jnp.logical_not(upward(f, c, du))
+
+        def second_onward(f, c, du, dv):
+            return upward(f, c, du, dv) if dv == 1 else jnp.logical_not(upward(f, c, du, dv))
+
+        def second_sem(f, du, dv):
+            return 16 + 4 * du + (dv - 1) + f
+
+        def own_second(c):
+            @pl.when(chip < 2 * row)
+            def _():
                 spread(0, 0, l_ref, own_a, c, g_ssem.at[0])
                 spread(1, 0, lall.at[own_b], own_b, c, g_ssem.at[1])
 
-            chunks(first_a)
-            chunks(first_b)
-            chunks(second)
-
-        def on_first(du, c, f):
+        chunks(own_second)
+
+        def first_arrival(du, c, f):
             block, live = block_of(f, du, 0)
 
             @pl.when(live)
             def _():
                 chunk_wait(block, c)
                 if du != 2:
-                    onward = upward(f, c, du) if du == 1 else jnp.logical_not(upward(f, c, du))
-
-                    @pl.when(onward)
+
+                    @pl.when(first_onward(f, c, du))
                     def _():
                         push(lall.at[block], block, c, g_ssem.at[4 * du + 2 + f], neighbour(f, du, 0))
 
+        def first_spread(du, c, f):
+            block, live = block_of(f, du, 0)
+
+            @pl.when(live)
+            def _():
                 spread(f, du, lall.at[block], block, c, g_ssem.at[4 * du + f])
 
-        def second_state(f, c, du, dv):
+        def on_second(du, dv, c, f):
             block, live = block_of(f, du, dv)
-            onward = upward(f, c, du, dv) if dv == 1 else jnp.logical_not(upward(f, c, du, dv))
-            return block, live & onward, 16 + 4 * du + (dv - 1) + f
-
-        def on_second(du, dv, c, f):
-            block, go, at = second_state(f, c, du, dv)
-
-            @pl.when(go)
+            at = second_sem(f, du, dv)
+
+            @pl.when(live & second_onward(f, c, du, dv))
             def _():
                 chunk_wait(block, c)
                 push(lall.at[block], block, c, g_ssem.at[at], neighbour(f, 0, dv, False))
@@ -315,8 +337,11 @@
 
         def first_both(c):
             for f in (0, 1):
-                on_first(1, c, f)
-                on_first(3, c, f)
+                first_arrival(1, c, f)
+                first_arrival(3, c, f)
+            for f in (0, 1):
+                first_spread(1, c, f)
+                first_spread(3, c, f)
 
         def second_of(*dus):
             def body(c):
@@ -329,7 +354,8 @@
 
         def first_far(c):
             for f in (0, 1):
-                on_first(2, c, f)
+                first_arrival(2, c, f)
+                first_spread(2, c, f)
 
         chunks(first_both)
         chunks(second_of(0))
@@ -340,15 +366,14 @@
         def sent(n, ssem):
             remote(lall.at[pl.ds(0, n)], lall.at[pl.ds(0, n)], ssem, o_rsem, me_chain).wait_send()
 
-        def some_sent(live, go, n, ssem):
-            @pl.when(live & by_chunk)
-            def _():
-                ref = lall.at[pl.ds(0, n), pl.ds(0, CB // 2)]
-                remote(ref, ref, ssem, o_rsem, me_chain).wait_send()
-
-            @pl.when(live & go & jnp.logical_not(by_chunk))
-            def _():
-                sent(n, ssem)
+        def some_sent(live, onward, n, ssem):
+            count = sum(onward(c).astype(jnp.int32) for c in range(CHUNKS))
+            for k in range(1, CHUNKS + 1):
+
+                @pl.when(live & (count == k))
+                def _():
+                    ref = lall.at[pl.ds(0, n), pl.ds(0, k * ROWS_C)]
+                    remote(ref, ref, ssem, o_rsem, me_chain).wait_send()
 
         for f in (0, 1):
 
@@ -364,14 +389,12 @@
                     sent(3, g_ssem.at[4 * du + f])
 
                 if du != 2:
-                    onward = upward(f, 0, du) if du == 1 else jnp.logical_not(upward(f, 0, du))
-                    some_sent(live, onward, 1, g_ssem.at[4 * du + 2 + f])
+                    some_sent(live, lambda c: first_onward(f, c, du), 1, g_ssem.at[4 * du + 2 + f])
 
             for du in range(4):
                 for dv in (1, 3):
                     live = block_of(f, du, dv)[1]
-                    _, go, at = second_state(f, 0, du, dv)
-                    some_sent(live, go, 2, g_ssem.at[at])
+                    some_sent(live, lambda c: second_onward(f, c, du, dv), 2, g_ssem.at[second_sem(f, du, dv)])
 
     @pl.when(is_gather)
     def _():

time: 48 us -> 47.3 us (0.985)
  no operation moved by 1% of the time
where the time goes in v6:
time: 47.3 us; the launch traced here: 47.2 us
  Pallas kernels  46.6 us (99%)
  local copies, waits for them, and re-layouts  0.62 us (1%)
    pallas_call x1, Pallas kernels, per_device(): pl.pallas_call(kernel, out_shape=pltpu.VMEM((NRHS, CB), F32), in_specs=[h...  46.6 us

profile of v6, /device:TPU:23, one launch (start us, length us, event | category | flops | bytes accessed | tf_op | source)
XLA Modules:
  0.0 47.2 jit_solution(11664084423597537009)
XLA Ops:
  0.0 46.6 %shard_map.46 = f32[64,128]{1,0:T(8,128)S(1)} custom-call(f32[64,512]{1,0:T(8,128)} %rhs_hbm.1, s32[1,4096]{1,0:T(1,128)} %bitcast.9, f32[512,128]{1,0:T(8,128)} %bitcast.8, f32[512,512]{1,0:T(8,128)} %bitcast.7), custom_call_target="tpu_custom_call" | custom-call | tf_op jit(solution)/shard_map/pallas_call | solution.py:544
  46.6 0.6 %copy.7 = f32[64,1,1,128]{3,2,1,0:T(1,128)} copy(f32[64,1,1,128]{3,2,1,0:T(1,128)S(1)} %bitcast.6) | data formatting | bytes 65536

commit v7 on v6

--- a/solution.py
+++ b/solution.py
@@ -20,7 +20,6 @@
 BF16, F32 = jnp.bfloat16, jnp.float32
 CHUNKS = 4
 ROWS_C = CB // CHUNKS
-PART = CB // CHIPS
 
 
 def split(v):
@@ -47,9 +46,9 @@
 
 def kernel(
     rhs_hbm, piv_hbm, l_hbm, d_hbm, out_ref,
-    rhs_ref, piv_ref, l_in, l_ref, d_ref, in_sem, s1_send, s1_recv, s2_send, s2_recv, e2, xhi, xlo, ybuf, acc, pbuf, orecv, lall, bhi, blo, dhi, dlo,
+    rhs_ref, piv_ref, l_in, l_ref, d_ref, in_sem, s1_part, s1_send, s1_recv, s2_send, s2_recv, e2, xhi, xlo, ybuf, acc, pbuf, orecv, lall, bhi, blo, dhi, dlo,
     s1_ssem, s1_rsem, s2_ssem, s2_rsem, y_ssem, y_rsem, o_ssem, o_rsem, g_ssem, g_rsem, b_ssem,
-    sc_ssem, u_rsem, w_rsem, c_rsem, un_ssem,
+    part_sem, meet_sem,
 ):
     row = lax.axis_index("row")
     col = lax.axis_index("col")
@@ -57,8 +56,6 @@
     x, y = chip // NY, chip % NY
     is_chain = core == CHAIN
     is_gather = core == GATHER
-    scattered = (row > 0) & (row <= 3)
-    relaying = row > 3
 
     def chain_col(c):
         return 2 * c + CHAIN
@@ -68,21 +65,27 @@
             src_ref=src, dst_ref=dst, send_sem=ssem, recv_sem=rsem, device_id=dev, device_id_type=MESH
         )
 
+    def at_xy(dx, dy):
+        return lax.rem(x + dx, NX) * NY + lax.rem(y + dy, NY)
+
+    around = [at_xy(1, 0), at_xy(3, 0), at_xy(0, 1), at_xy(0, 3)]
+    above, below = lax.rem(row + 1, ROWS), lax.rem(row + ROWS - 1, ROWS)
+
     barrier = pltpu.get_barrier_semaphore()
 
-    def greet_plane(i, _):
-        pl.semaphore_signal(barrier, inc=1, device_id=(row, lax.rem(col + i, COLS)), device_id_type=MESH)
-        return 0
-
-    def greet_z(i, _):
-        pl.semaphore_signal(barrier, inc=1, device_id=(lax.rem(row + i, ROWS), col), device_id_type=MESH)
-        return 0
-
-    lax.fori_loop(1, COLS, greet_plane, 0)
+    def greet(r, c):
+        pl.semaphore_signal(barrier, inc=1, device_id=(r, c), device_id_type=MESH)
+
+    greet(row, 2 * chip + 1 - core)
+    for c in around:
+        greet(row, 2 * c + GATHER)
 
     @pl.when(is_chain)
     def _():
-        lax.fori_loop(1, ROWS, greet_z, 0)
+        for c in around:
+            greet(row, 2 * c + CHAIN)
+        greet(above, col)
+        greet(below, col)
 
     load_rhs = pltpu.make_async_copy(rhs_hbm, rhs_ref, in_sem.at[0])
     load_l = pltpu.make_async_copy(l_hbm, l_in, in_sem.at[1])
@@ -106,56 +109,16 @@
     load_l.wait()
     l_ref[...] = l_in[...].T
 
-    @pl.when(is_gather & scattered)
-    def _():
-        part = pl.ds(pl.multiple_of(chip * PART, PART), PART)
-        lall[col, part] = l_ref[part]
-
     @pl.when(is_chain)
     def _():
-        load_piv.wait()
-        load_d.wait()
-        pl.semaphore_wait(barrier, COLS - 1 + ROWS - 1)
+        pl.semaphore_wait(barrier, 1 + 4 + 2)
 
     @pl.when(is_gather)
     def _():
-        pl.semaphore_wait(barrier, COLS - 1)
-
-    def scatter(ssem):
-        m, f = jnp.minimum(chip // 2, 2), lax.rem(chip, 2)
-
-        def one(i, _):
-            c = lax.rem(chip + i, CHIPS)
-            part = pl.ds(pl.multiple_of(c * PART, PART), PART)
-            remote(l_ref.at[part], lall.at[col, part], ssem, u_rsem.at[m, f], (row, 2 * c + GATHER)).start()
-            return 0
-
-        return one
+        pl.semaphore_wait(barrier, 1 + 8)
 
     own_live = chip < 2 * row
-
-    @pl.when(own_live & scattered & is_gather)
-    def _():
-        lax.fori_loop(1, CHIPS, scatter(sc_ssem), 0)
-
-    @pl.when(own_live & scattered & is_chain)
-    def _():
-        lax.fori_loop(0, CHIPS, scatter(b_ssem), 0)
-
-    def send_s1(i, _):
-        c = lax.rem(chip + i, CHIPS)
-        remote(s1_send.at[c], s1_recv.at[col], s1_ssem, s1_rsem, (row, chain_col(c))).start()
-        return 0
-
-    @pl.when(is_gather)
-    def _():
-        lax.fori_loop(0, CHIPS, send_s1, 0)
-
-    @pl.when(is_chain)
-    def _():
-        s1_recv[col] = s1_send[chip]
-        lax.fori_loop(1, CHIPS, send_s1, 0)
-
+    partner = (row, 2 * chip + 1 - core)
     me_chain = (row, chain_col(chip))
 
 
@@ -170,15 +133,15 @@
         u, v = place(f)
         first = lax.rem(u - du + NX, NX)
         if dv is None:
-            odd = lax.rem(first + c, 2) == 1
+            odd = lax.rem(first + jnp.where(row == 1, 0, c), 2) == 1
             along_x, at_x = f == 0, first
         else:
             second = lax.rem(v - dv + NY, NY)
-            odd = lax.rem(first + second + c, 2) == 1
+            odd = lax.rem(second + jnp.where(row == 1, 0, first + c), 2) == 1
             along_x, at_x = f == 1, second
         if not along_x:
             return odd
-        uneven = (at_x == 2) | ((at_x == 1) & ((row == 4) | (c != 0)))
+        uneven = (at_x == 2) | ((at_x == 1) & ((row <= 4) | (c != 0)))
         return ((row >= 6) & odd) | ((row < 6) & uneven)
 
     def block_of(f, du, dv):
@@ -210,69 +173,10 @@
 
         lax.fori_loop(0, CHUNKS, one, 0)
 
-    def unit(c, f, m):
-        return lall.at[pl.ds(4 * m + 2 * f, 2), pl.ds(pl.multiple_of(c * PART, PART), PART)]
-
-    def unit_of(f, du):
-        return flow_chip(f, (4 - du) % 4, 0)
-
-    def unit_send(c, f, m, rsem, dev):
-        remote(unit(c, f, m), unit(c, f, m), un_ssem.at[m], rsem, dev).start()
-
-    def unit_spread(c, f, m):
-        unit_send(c, f, m, c_rsem.at[m], me_chain)
-        for dv in (2, 3, 1):
-            unit_send(c, f, m, c_rsem.at[m], (row, chain_col(flow_chip(f, 0, dv))))
-
-    @pl.when(is_gather & scattered)
-    def _():
-        def own_units(m, _):
-            for f in (0, 1):
-                ref = lall.at[pl.ds(4 * m + 2 * f, 2), pl.ds(0, PART)]
-                one = lall.at[pl.ds(4 * m + 2 * f, 1), pl.ds(0, PART)]
-
-                @pl.when(chip == 2 * m + f)
-                def _():
-                    remote(one, one, b_ssem, u_rsem.at[m, f], me_chain).wait_recv()
-
-                @pl.when(chip != 2 * m + f)
-                def _():
-                    remote(ref, ref, b_ssem, u_rsem.at[m, f], me_chain).wait_recv()
-
-                for du in (2, 1, 3):
-                    unit_send(chip, f, m, w_rsem.at[du, m, f], (row, 2 * flow_chip(f, du, 0) + GATHER))
-            return 0
-
-        def own_spread(m, _):
-            for f in (0, 1):
-                unit_spread(chip, f, m)
-            return 0
-
-        def relay_units(m, _):
-            for du in (1, 3, 2):
-                for f in (0, 1):
-                    c = unit_of(f, du)
-                    remote(unit(c, f, m), unit(c, f, m), b_ssem, w_rsem.at[du, m, f], me_chain).wait_recv()
-                    unit_spread(c, f, m)
-            return 0
-
-        def units_sent(m, _):
-            ref = lall.at[pl.ds(0, 19), pl.ds(0, 4 * PART)]
-            remote(ref, ref, un_ssem.at[m], o_rsem, me_chain).wait_send()
-            return 0
-
-        lax.fori_loop(0, row, own_units, 0)
-        lax.fori_loop(0, row, own_spread, 0)
-        lax.fori_loop(0, row, relay_units, 0)
-        lax.fori_loop(0, row, units_sent, 0)
-
-        @pl.when(chip < 2 * row)
-        def _():
-            ref = l_ref.at[pl.ds(0, CB - PART)]
-            remote(ref, ref, sc_ssem, o_rsem, me_chain).wait_send()
-
-    @pl.when(is_gather & relaying)
-    def _():
+    @pl.when(is_gather)
+    def _():
+        remote(s1_send, s1_part, s1_ssem, part_sem, me_chain).start()
+
         own_a, own_b = 2 * chip, 2 * chip + 1
 
         @pl.when(chip < 2 * row)
@@ -403,22 +307,62 @@
 
     @pl.when(is_chain)
     def _():
-        partner = (row, 2 * chip + GATHER)
-        @pl.when(own_live & relaying)
+        def tell(k, a, b):
+            for dev in (a, b):
+                pl.semaphore_signal(meet_sem.at[k], inc=1, device_id=dev, device_id_type=MESH)
+
+        def hear(k):
+            pl.semaphore_wait(meet_sem.at[k], 2)
+
+        x_sides = [(row, chain_col(c)) for c in around[:2]]
+        y_sides = [(row, chain_col(c)) for c in around[2:]]
+        z_sides = [(above, col), (below, col)]
+
+        tell(0, *x_sides)
+        tell(3, *z_sides)
+
+        @pl.when(own_live)
         def _():
             chunks(lambda c: push(l_ref, 2 * chip + CHAIN, c, b_ssem, partner))
+
+        hear(0)
+        tell(1, *y_sides)
+        hear(1)
+        tell(2, *y_sides)
+        hear(2)
+
+        remote(s1_part, s1_part, b_ssem, part_sem, partner).wait_recv()
+
+        def send_s1(i, _):
+            c = lax.rem(chip + i, CHIPS)
+            remote(s1_send.at[c], s1_recv.at[col], s1_ssem, s1_rsem, (row, chain_col(c))).start()
+            remote(s1_part.at[c], s1_recv.at[2 * chip + GATHER], s1_ssem, s1_rsem, (row, chain_col(c))).start()
+            return 0
+
+        lax.fori_loop(1, CHIPS, send_s1, 0)
+        s1_recv[col] = s1_send[chip]
+        s1_recv[2 * chip + GATHER] = s1_part[chip]
+        hear(3)
+        tell(4, *z_sides)
+        load_d.wait()
+        load_piv.wait()
 
         d = d_ref[...].T
         hi, lo = split(d)
         dhi[...] = hi
         dlo[...] = lo
 
+        hear(4)
+        tell(5, *z_sides)
+
         width = COLS * BLK
         piv = piv_ref[...] - row * width
         low = jnp.broadcast_to(piv & (2 * CB - 1), (2 * CB, ROWS * BLK))
         e2[...] = (lax.broadcasted_iota(jnp.int32, (2 * CB, ROWS * BLK), 0) == low).astype(F32).astype(BF16)
 
-        remote(s1_recv.at[pl.ds(0, COLS - 1)], s1_recv.at[pl.ds(0, COLS - 1)], b_ssem, s1_rsem, partner).wait_recv()
+        hear(5)
+        others = s1_recv.at[pl.ds(0, COLS - 2)]
+        remote(others, others, b_ssem, s1_rsem, partner).wait_recv()
         for h in range(2):
             v = s1_recv[:, 2 * G * h : 2 * G * h + 2 * G, :].reshape(COLS * 2 * G, CB)
             hi, lo = split(v)
@@ -465,15 +409,8 @@
         def step(m, _):
             @pl.when(m < row)
             def _():
-                @pl.when(relaying)
-                def _():
-                    for t in range(4):
-                        chunks(lambda c: chunk_wait(4 * m + t, c))
-
-                @pl.when(scattered)
-                def _():
-                    four = lall.at[pl.ds(4 * m, 4)]
-                    remote(four, four, b_ssem, c_rsem.at[m], partner).wait_recv()
+                for t in range(4):
+                    chunks(lambda c: chunk_wait(4 * m + t, c))
 
                 for t in range(4):
                     hi, lo = split(lall[4 * m + t])
@@ -512,7 +449,7 @@
         def _():
             remote(l_ref, l_ref, b_ssem, o_rsem, partner).wait_send()
 
-        remote(s1_send.at[pl.ds(0, CHIPS - 1)], s1_send.at[pl.ds(0, CHIPS - 1)], s1_ssem, s1_rsem, partner).wait_send()
+        remote(others, others, s1_ssem, s1_rsem, partner).wait_send()
         remote(s2_send.at[pl.ds(0, ROWS - 1)], s2_send.at[pl.ds(0, ROWS - 1)], s2_ssem, s2_rsem, partner).wait_send()
         remote(ybuf.at[pl.ds(0, ROWS - 1)], ybuf.at[pl.ds(0, ROWS - 1)], y_ssem, y_rsem.at[row], partner).wait_send()
 
@@ -553,6 +490,7 @@
             pltpu.VMEM((CB, BLK), F32),
             pltpu.VMEM((BLK, BLK), F32),
             dma((4,)),
+            pltpu.VMEM((CHIPS, 4 * G, CB), F32),
             pltpu.VMEM((CHIPS, 4 * G, CB), F32),
             pltpu.VMEM((COLS, 4 * G, CB), F32),
             pltpu.VMEM((ROWS, 8, BLK // 2), F32),
@@ -577,10 +515,7 @@
             dma((COLS, CHUNKS)),
             dma,
             dma,
-            dma((3, 2)),
-            dma((4, 3, 2)),
-            dma((3,)),
-            dma((3,)),
+            pltpu.SemaphoreType.REGULAR((6,)),
         ],
         compiler_params=pltpu.CompilerParams(
             collective_id=0, has_side_effects=True, vmem_limit_bytes=55200 * 1024

time: 47.3 us -> 46.8 us (0.989)
  Pallas kernels: 46.6 us -> 46.1 us
    pallas_call x1, Pallas kernels: 46.6 us -> 46.1 us  [per_device(): pl.pallas_call(kernel, out_shape=pltpu.VMEM((NRHS, CB), F32), in_specs=[h...]
where the time goes in v7:
time: 46.8 us; the launch traced here: 46.7 us
  Pallas kernels  46.1 us (99%)
  local copies, waits for them, and re-layouts  0.62 us (1%)
    pallas_call x1, Pallas kernels, per_device(): pl.pallas_call(kernel, out_shape=pltpu.VMEM((NRHS, CB), F32), in_specs=[h...  46.1 us

profile of v7, /device:TPU:23, one launch (start us, length us, event | category | flops | bytes accessed | tf_op | source)
XLA Modules:
  0.0 46.7 jit_solution(11968201931686148280)
XLA Ops:
  0.0 46.1 %shard_map.46 = f32[64,128]{1,0:T(8,128)S(1)} custom-call(f32[64,512]{1,0:T(8,128)} %rhs_hbm.1, s32[1,4096]{1,0:T(1,128)} %bitcast.9, f32[512,128]{1,0:T(8,128)} %bitcast.8, f32[512,512]{1,0:T(8,128)} %bitcast.7), custom_call_target="tpu_custom_call" | custom-call | tf_op jit(solution)/shard_map/pallas_call | solution.py:481
  46.1 0.6 %copy.7 = f32[64,1,1,128]{3,2,1,0:T(1,128)} copy(f32[64,1,1,128]{3,2,1,0:T(1,128)S(1)} %bitcast.6) | data formatting | bytes 65536

commit v8 on v7

--- a/solution.py
+++ b/solution.py
@@ -69,6 +69,8 @@
         return lax.rem(x + dx, NX) * NY + lax.rem(y + dy, NY)
 
     around = [at_xy(1, 0), at_xy(3, 0), at_xy(0, 1), at_xy(0, 3)]
+    x_ring = [at_xy(i, 0) for i in (1, 3, 2)]
+    y_ring = [at_xy(0, i) for i in (1, 3, 2)]
     above, below = lax.rem(row + 1, ROWS), lax.rem(row + ROWS - 1, ROWS)
 
     barrier = pltpu.get_barrier_semaphore()
@@ -80,10 +82,15 @@
     for c in around:
         greet(row, 2 * c + GATHER)
 
+    @pl.when(is_gather)
+    def _():
+        for c in around:
+            greet(row, chain_col(c))
+
     @pl.when(is_chain)
     def _():
-        for c in around:
-            greet(row, 2 * c + CHAIN)
+        for c in x_ring + y_ring:
+            greet(row, chain_col(c))
         greet(above, col)
         greet(below, col)
 
@@ -111,7 +118,7 @@
 
     @pl.when(is_chain)
     def _():
-        pl.semaphore_wait(barrier, 1 + 4 + 2)
+        pl.semaphore_wait(barrier, 1 + 4 + 6 + 2)
 
     @pl.when(is_gather)
     def _():
@@ -122,45 +129,48 @@
     me_chain = (row, chain_col(chip))
 
 
-    def flow_chip(f, du, dv):
-        dx, dy = (du, dv) if f == 0 else (dv, du)
-        return lax.rem(x + dx, NX) * NY + lax.rem(y + dy, NY)
-
-    def place(f):
-        return (x, y) if f == 0 else (y, x)
+    def x_first(f, c):
+        return True if f == 0 else (row == 2) & (c < 2)
+
+    def either(f, c, a, b):
+        return a if f == 0 else jnp.where(x_first(f, c), a, b)
+
+    def flow_chip(f, c, du, dv):
+        return at_xy(either(f, c, du, dv), either(f, c, dv, du))
 
     def upward(f, c, du, dv=None):
-        u, v = place(f)
-        first = lax.rem(u - du + NX, NX)
+        first = lax.rem(either(f, c, x, y) - du + NX, NX)
         if dv is None:
+            at = first
             odd = lax.rem(first + jnp.where(row == 1, 0, c), 2) == 1
-            along_x, at_x = f == 0, first
         else:
-            second = lax.rem(v - dv + NY, NY)
-            odd = lax.rem(second + jnp.where(row == 1, 0, first + c), 2) == 1
-            along_x, at_x = f == 1, second
-        if not along_x:
-            return odd
-        uneven = (at_x == 2) | ((at_x == 1) & ((row <= 4) | (c != 0)))
-        return ((row >= 6) & odd) | ((row < 6) & uneven)
-
-    def block_of(f, du, dv):
-        c = flow_chip(f, (4 - du) % 4, (4 - dv) % 4)
-        return 2 * c + f, c < 2 * row
+            at = lax.rem(either(f, c, y, x) - dv + NY, NY)
+            odd = lax.rem(at + jnp.where(row == 1, 0, first + c), 2) == 1
+        uneven = (at == 2) | ((at == 1) & ((row <= 4) | (c != 0)))
+        by_x = ((row >= 6) & odd) | ((row < 6) & uneven)
+        if f == 0:
+            return by_x if dv is None else odd
+        along_x = x_first(f, c) if dv is None else jnp.logical_not(x_first(f, c))
+        return (along_x & by_x) | (jnp.logical_not(along_x) & odd)
+
+    def block_of(f, c, du, dv):
+        a = flow_chip(f, c, (4 - du) % 4, (4 - dv) % 4)
+        return 2 * a + f, a < 2 * row
 
     def push(src, block, c, ssem, dev):
         part = pl.ds(c * ROWS_C, ROWS_C)
         remote(src.at[part], lall.at[block, part], ssem, g_rsem.at[block, c], dev).start()
 
-    def neighbour(f, du, dv, relayed=True):
+    def neighbour(f, c, du, dv, relayed=True):
         role = jnp.where(relayed, GATHER, CHAIN) if not isinstance(relayed, bool) else (GATHER if relayed else CHAIN)
-        return (row, flow_chip(f, du, dv) * 2 + role)
-
-    def spread(f, du, src, block, c, ssem):
+        return (row, flow_chip(f, c, du, dv) * 2 + role)
+
+    def spread(f, du, src, block, c, ssem, home=True):
         plus = upward(f, c, du, 0)
-        push(src, block, c, ssem, neighbour(f, 0, 1, plus))
-        push(src, block, c, ssem, neighbour(f, 0, 3, jnp.logical_not(plus)))
-        push(src, block, c, ssem, me_chain)
+        if home:
+            push(src, block, c, ssem, me_chain)
+        push(src, block, c, ssem, neighbour(f, c, 0, 1, plus))
+        push(src, block, c, ssem, neighbour(f, c, 0, 3, jnp.logical_not(plus)))
 
     def chunk_wait(block, c):
         part = pl.ds(c * ROWS_C, ROWS_C)
@@ -177,21 +187,21 @@
     def _():
         remote(s1_send, s1_part, s1_ssem, part_sem, me_chain).start()
 
-        own_a, own_b = 2 * chip, 2 * chip + 1
+        own = 2 * chip + GATHER
 
         @pl.when(chip < 2 * row)
         def _():
-            def first_a(c):
-                push(l_ref, own_a, c, g_ssem.at[0], neighbour(0, 1, 0))
-                push(l_ref, own_a, c, g_ssem.at[0], neighbour(0, 3, 0))
-
-            def first_b(c):
-                chunk_wait(own_b, c)
-                push(lall.at[own_b], own_b, c, g_ssem.at[1], neighbour(1, 1, 0))
-                push(lall.at[own_b], own_b, c, g_ssem.at[1], neighbour(1, 3, 0))
-
-            chunks(first_a)
-            chunks(first_b)
+            def first(c):
+                push(l_ref, own, c, g_ssem.at[0], neighbour(0, c, 1, 0))
+                push(l_ref, own, c, g_ssem.at[0], neighbour(0, c, 3, 0))
+
+            def second(c):
+                spread(0, 0, l_ref, own, c, g_ssem.at[0])
+                chunk_wait(own + 1, c)
+                spread(1, 0, lall.at[own + 1], own + 1, c, g_ssem.at[1], False)
+
+            chunks(first)
+            chunks(second)
 
         def first_onward(f, c, du):
             return upward(f, c, du) if du == 1 else jnp.logical_not(upward(f, c, du))
@@ -202,16 +212,8 @@
         def second_sem(f, du, dv):
             return 16 + 4 * du + (dv - 1) + f
 
-        def own_second(c):
-            @pl.when(chip < 2 * row)
-            def _():
-                spread(0, 0, l_ref, own_a, c, g_ssem.at[0])
-                spread(1, 0, lall.at[own_b], own_b, c, g_ssem.at[1])
-
-        chunks(own_second)
-
         def first_arrival(du, c, f):
-            block, live = block_of(f, du, 0)
+            block, live = block_of(f, c, du, 0)
 
             @pl.when(live)
             def _():
@@ -220,23 +222,23 @@
 
                     @pl.when(first_onward(f, c, du))
                     def _():
-                        push(lall.at[block], block, c, g_ssem.at[4 * du + 2 + f], neighbour(f, du, 0))
+                        push(lall.at[block], block, c, g_ssem.at[4 * du + 2 + f], neighbour(f, c, du, 0))
 
         def first_spread(du, c, f):
-            block, live = block_of(f, du, 0)
+            block, live = block_of(f, c, du, 0)
 
             @pl.when(live)
             def _():
                 spread(f, du, lall.at[block], block, c, g_ssem.at[4 * du + f])
 
         def on_second(du, dv, c, f):
-            block, live = block_of(f, du, dv)
+            block, live = block_of(f, c, du, dv)
             at = second_sem(f, du, dv)
 
             @pl.when(live & second_onward(f, c, du, dv))
             def _():
                 chunk_wait(block, c)
-                push(lall.at[block], block, c, g_ssem.at[at], neighbour(f, 0, dv, False))
+                push(lall.at[block], block, c, g_ssem.at[at], neighbour(f, c, 0, dv, False))
                 push(lall.at[block], block, c, g_ssem.at[at], me_chain)
 
         def first_both(c):
@@ -267,38 +269,31 @@
         chunks(second_of(1, 3))
         chunks(second_of(2))
 
-        def sent(n, ssem):
-            remote(lall.at[pl.ds(0, n)], lall.at[pl.ds(0, n)], ssem, o_rsem, me_chain).wait_send()
-
-        def some_sent(live, onward, n, ssem):
-            count = sum(onward(c).astype(jnp.int32) for c in range(CHUNKS))
+        def some_sent(went, n, ssem):
+            count = sum(went(c).astype(jnp.int32) for c in range(CHUNKS))
             for k in range(1, CHUNKS + 1):
 
-                @pl.when(live & (count == k))
+                @pl.when(count == k)
                 def _():
                     ref = lall.at[pl.ds(0, n), pl.ds(0, k * ROWS_C)]
                     remote(ref, ref, ssem, o_rsem, me_chain).wait_send()
 
+        def live_chunk(f, du, dv):
+            return lambda c: block_of(f, c, du, dv)[1]
+
         for f in (0, 1):
-
-            @pl.when(chip < 2 * row)
-            def _():
-                sent(5, g_ssem.at[f])
+            some_sent(lambda c: chip < 2 * row, 2 if f == CHAIN else 5, g_ssem.at[f])
 
             for du in (1, 2, 3):
-                block, live = block_of(f, du, 0)
-
-                @pl.when(live)
-                def _():
-                    sent(3, g_ssem.at[4 * du + f])
-
+                live = live_chunk(f, du, 0)
+                some_sent(live, 3, g_ssem.at[4 * du + f])
                 if du != 2:
-                    some_sent(live, lambda c: first_onward(f, c, du), 1, g_ssem.at[4 * du + 2 + f])
+                    some_sent(lambda c: live(c) & first_onward(f, c, du), 1, g_ssem.at[4 * du + 2 + f])
 
             for du in range(4):
                 for dv in (1, 3):
-                    live = block_of(f, du, dv)[1]
-                    some_sent(live, lambda c: second_onward(f, c, du, dv), 2, g_ssem.at[second_sem(f, du, dv)])
+                    live = live_chunk(f, du, dv)
+                    some_sent(lambda c: live(c) & second_onward(f, c, du, dv), 2, g_ssem.at[second_sem(f, du, dv)])
 
     @pl.when(is_gather)
     def _():
@@ -307,29 +302,29 @@
 
     @pl.when(is_chain)
     def _():
-        def tell(k, a, b):
-            for dev in (a, b):
+        def tell(k, devs):
+            for dev in devs:
                 pl.semaphore_signal(meet_sem.at[k], inc=1, device_id=dev, device_id_type=MESH)
 
-        def hear(k):
-            pl.semaphore_wait(meet_sem.at[k], 2)
-
-        x_sides = [(row, chain_col(c)) for c in around[:2]]
-        y_sides = [(row, chain_col(c)) for c in around[2:]]
+        def hear(k, n):
+            pl.semaphore_wait(meet_sem.at[k], n)
+
         z_sides = [(above, col), (below, col)]
 
-        tell(0, *x_sides)
-        tell(3, *z_sides)
+        tell(0, [(row, chain_col(c)) for c in y_ring])
+        tell(1, z_sides)
 
         @pl.when(own_live)
         def _():
-            chunks(lambda c: push(l_ref, 2 * chip + CHAIN, c, b_ssem, partner))
-
-        hear(0)
-        tell(1, *y_sides)
-        hear(1)
-        tell(2, *y_sides)
-        hear(2)
+            def first(c):
+                push(l_ref, col, c, b_ssem, neighbour(1, c, 1, 0))
+                push(l_ref, col, c, b_ssem, neighbour(1, c, 3, 0))
+                push(l_ref, col, c, b_ssem, partner)
+
+            chunks(first)
+            lall[col] = l_ref[...]
+
+        hear(0, 3)
 
         remote(s1_part, s1_part, b_ssem, part_sem, partner).wait_recv()
 
@@ -342,8 +337,8 @@
         lax.fori_loop(1, CHIPS, send_s1, 0)
         s1_recv[col] = s1_send[chip]
         s1_recv[2 * chip + GATHER] = s1_part[chip]
-        hear(3)
-        tell(4, *z_sides)
+        hear(1, 2)
+        tell(2, z_sides)
         load_d.wait()
         load_piv.wait()
 
@@ -352,15 +347,15 @@
         dhi[...] = hi
         dlo[...] = lo
 
-        hear(4)
-        tell(5, *z_sides)
+        hear(2, 2)
+        tell(3, z_sides)
 
         width = COLS * BLK
         piv = piv_ref[...] - row * width
         low = jnp.broadcast_to(piv & (2 * CB - 1), (2 * CB, ROWS * BLK))
         e2[...] = (lax.broadcasted_iota(jnp.int32, (2 * CB, ROWS * BLK), 0) == low).astype(F32).astype(BF16)
 
-        hear(5)
+        hear(3, 2)
         others = s1_recv.at[pl.ds(0, COLS - 2)]
         remote(others, others, b_ssem, s1_rsem, partner).wait_recv()
         for h in range(2):
@@ -396,23 +391,25 @@
         pbuf[...] = unpacked(jnp.sum(s2_recv[...], axis=0))
         acc[...] = jnp.zeros_like(acc)
 
-        def finish():
-            fresh = times(pbuf[...] - acc[...], dhi, dlo)
+        def finish(summed):
+            fresh = times(pbuf[...] - summed, dhi, dlo)
             ybuf[row] = packed(fresh)
             for i in range(1, ROWS):
                 remote(ybuf.at[row], ybuf.at[row], y_ssem, y_rsem.at[row], (lax.rem(row + i, ROWS), col)).start()
 
         @pl.when(row == 0)
         def _():
-            finish()
+            finish(acc[...])
 
         def step(m, _):
             @pl.when(m < row)
             def _():
                 for t in range(4):
-                    chunks(lambda c: chunk_wait(4 * m + t, c))
-
-                for t in range(4):
+
+                    @pl.when(4 * m + t != col)
+                    def _():
+                        chunks(lambda c: chunk_wait(4 * m + t, c))
+
                     hi, lo = split(lall[4 * m + t])
                     bhi[CB * t : CB * t + CB, :] = hi
                     blo[CB * t : CB * t + CB, :] = lo
@@ -421,13 +418,13 @@
             def _():
                 remote(ybuf.at[m], ybuf.at[m], b_ssem, y_rsem.at[m], partner).wait_recv()
 
-            @pl.when(m < row)
+            @pl.when(m + 1 < row)
             def _():
                 acc[...] += times(unpacked(ybuf[m]), bhi, blo)
 
             @pl.when(m + 1 == row)
             def _():
-                finish()
+                finish(acc[...] + times(unpacked(ybuf[m]), bhi, blo))
 
             for t in range(4):
                 lanes = pl.ds(CB * (t % 2), CB)
@@ -447,7 +444,8 @@
 
         @pl.when(own_live)
         def _():
-            remote(l_ref, l_ref, b_ssem, o_rsem, partner).wait_send()
+            three = lall.at[pl.ds(0, 3)]
+            remote(three, three, b_ssem, o_rsem, partner).wait_send()
 
         remote(others, others, s1_ssem, s1_rsem, partner).wait_send()
         remote(s2_send.at[pl.ds(0, ROWS - 1)], s2_send.at[pl.ds(0, ROWS - 1)], s2_ssem, s2_rsem, partner).wait_send()
@@ -515,7 +513,7 @@
             dma((COLS, CHUNKS)),
             dma,
             dma,
-            pltpu.SemaphoreType.REGULAR((6,)),
+            pltpu.SemaphoreType.REGULAR((4,)),
         ],
         compiler_params=pltpu.CompilerParams(
             collective_id=0, has_side_effects=True, vmem_limit_bytes=55200 * 1024

time: 46.8 us -> 46.7 us (level); the launches traced: 46.7 us -> 46.2 us
  Pallas kernels: 46.1 us -> 45.6 us
    pallas_call x1, Pallas kernels: 46.1 us -> 45.6 us  [per_device(): pl.pallas_call(kernel, out_shape=pltpu.VMEM((NRHS, CB), F32), in_specs=[h...]
where the time goes in v8:
time: 46.7 us; the launch traced here: 46.2 us
  Pallas kernels  45.6 us (98%)
  local copies, waits for them, and re-layouts  0.62 us (1%)
    pallas_call x1, Pallas kernels, per_device(): pl.pallas_call(kernel, out_shape=pltpu.VMEM((NRHS, CB), F32), in_specs=[h...  45.6 us

profile of v8, /device:TPU:23, one launch (start us, length us, event | category | flops | bytes accessed | tf_op | source)
XLA Modules:
  0.0 46.2 jit_solution(5160754033318828561)
XLA Ops:
  0.0 45.6 %shard_map.46 = f32[64,128]{1,0:T(8,128)S(1)} custom-call(f32[64,512]{1,0:T(8,128)} %rhs_hbm.1, s32[1,4096]{1,0:T(1,128)} %bitcast.9, f32[512,128]{1,0:T(8,128)} %bitcast.8, f32[512,512]{1,0:T(8,128)} %bitcast.7), custom_call_target="tpu_custom_call" | custom-call | tf_op jit(solution)/shard_map/pallas_call | solution.py:479
  45.6 0.6 %copy.7 = f32[64,1,1,128]{3,2,1,0:T(1,128)} copy(f32[64,1,1,128]{3,2,1,0:T(1,128)S(1)} %bitcast.6) | data formatting | bytes 65536

commit v9 on v8

--- a/solution.py
+++ b/solution.py
@@ -18,7 +18,7 @@
 G = NRHS // CHIPS
 CHAIN, GATHER = 1, 0
 BF16, F32 = jnp.bfloat16, jnp.float32
-CHUNKS = 4
+CHUNKS = 2
 ROWS_C = CB // CHUNKS
 
 
@@ -130,7 +130,7 @@
 
 
     def x_first(f, c):
-        return True if f == 0 else (row == 2) & (c < 2)
+        return True if f == 0 else (row == 2) & (c < 1)
 
     def either(f, c, a, b):
         return a if f == 0 else jnp.where(x_first(f, c), a, b)

time: 46.7 us -> 46.3 us (level)
  no operation moved by 1% of the time
where the time goes in v9:
time: 46.3 us; the launch traced here: 45.8 us
  Pallas kernels  45.2 us (98%)
  local copies, waits for them, and re-layouts  0.62 us (1%)
    pallas_call x1, Pallas kernels, per_device(): pl.pallas_call(kernel, out_shape=pltpu.VMEM((NRHS, CB), F32), in_specs=[h...  45.2 us

profile of v9, /device:TPU:23, one launch (start us, length us, event | category | flops | bytes accessed | tf_op | source)
XLA Modules:
  0.0 45.8 jit_solution(7584080548774577371)
XLA Ops:
  0.0 45.2 %shard_map.46 = f32[64,128]{1,0:T(8,128)S(1)} custom-call(f32[64,512]{1,0:T(8,128)} %rhs_hbm.1, s32[1,4096]{1,0:T(1,128)} %bitcast.9, f32[512,128]{1,0:T(8,128)} %bitcast.8, f32[512,512]{1,0:T(8,128)} %bitcast.7), custom_call_target="tpu_custom_call" | custom-call | tf_op jit(solution)/shard_map/pallas_call | solution.py:479
  45.2 0.6 %copy.7 = f32[64,1,1,128]{3,2,1,0:T(1,128)} copy(f32[64,1,1,128]{3,2,1,0:T(1,128)S(1)} %bitcast.6) | data formatting | bytes 65536

commit v10 on v9

--- a/solution.py
+++ b/solution.py
@@ -130,7 +130,7 @@
 
 
     def x_first(f, c):
-        return True if f == 0 else (row == 2) & (c < 1)
+        return True if f == 0 else ((row == 2) | (row == 3)) & (c < 1)
 
     def either(f, c, a, b):
         return a if f == 0 else jnp.where(x_first(f, c), a, b)

time: 46.3 us -> 46.3 us (level)
  no operation moved by 1% of the time
where the time goes in v10:
time: 46.3 us; the launch traced here: 45.8 us
  Pallas kernels  45.2 us (98%)
  local copies, waits for them, and re-layouts  0.62 us (1%)
    pallas_call x1, Pallas kernels, per_device(): pl.pallas_call(kernel, out_shape=pltpu.VMEM((NRHS, CB), F32), in_specs=[h...  45.2 us

profile of v10, /device:TPU:23, one launch (start us, length us, event | category | flops | bytes accessed | tf_op | source)
XLA Modules:
  0.0 45.8 jit_solution(14624292073488554618)
XLA Ops:
  0.0 45.2 %shard_map.46 = f32[64,128]{1,0:T(8,128)S(1)} custom-call(f32[64,512]{1,0:T(8,128)} %rhs_hbm.1, s32[1,4096]{1,0:T(1,128)} %bitcast.9, f32[512,128]{1,0:T(8,128)} %bitcast.8, f32[512,512]{1,0:T(8,128)} %bitcast.7), custom_call_target="tpu_custom_call" | custom-call | tf_op jit(solution)/shard_map/pallas_call | solution.py:479
  45.2 0.6 %copy.7 = f32[64,1,1,128]{3,2,1,0:T(1,128)} copy(f32[64,1,1,128]{3,2,1,0:T(1,128)S(1)} %bitcast.6) | data formatting | bytes 65536
